TPU v7x, 1024 devices: a whole 4x4x32 slice. The times are simulated.
1024 devices in a mesh: gx: 8 (over z_hi, core), gy: 4 (over x), gz: 32 (over z_lo, y).
Axes of the slice: x: 4, y: 4, z: 32 (z_hi: 4, z_lo: 8; z = z_hi * 8 + z_lo), core: 2. Of those that a mesh axis runs over, the one named last changes fastest.
Arguments:
- euler_state: float32 [5, 32, 32, 4096], P(None, 'gx', 'gy', 'gz'), as said below
- gravity_state: float32 [4, 32, 32, 4096], P(None, 'gx', 'gy', 'gz'), may hold values from -6 to 6
Outputs:
- section_rate: float32 [5, 32, 32, 4096], P(None, 'gx', 'gy', 'gz')
- gravity_next: float32 [4, 32, 32, 4096], P(None, 'gx', 'gy', 'gz')
- gravity_source: float32 [4, 32, 32, 4096], P(None, 'gx', 'gy', 'gz')
- residual_norm: float32 [], replicated
Inputs may be any that keep to these rules, and one draw needn't show every extreme that they name: `euler_state`: each node's density lies between 0.7 and 3.9 and its pressure, for a ratio of specific heats of 1.4, between 0.7 and 71.
All inputs are finite; a program needn't handle non-finite values.
Results may differ from a plain program's by a relative error of at most 0.0003.
Values sent between devices are 32-bit elements; how exact they have to be, the bound alone decides.
No kernel may reach another device: no remote copies, remote signals or barrier semaphores. Data moves between devices by JAX's collectives and lax.ppermute only.
A program may use at most 32 MiB of HBM per device.

v0:
```python
import functools
import math

import jax
import jax.numpy as jnp
import numpy as np
from jax import lax
from jax.experimental import pallas as pl
from jax.experimental.pallas import tpu as pltpu
from jax.sharding import Mesh
from jax.sharding import PartitionSpec as P


ITERS = 3
GX = ("gx_0", "gx_1")
GZ = ("gz_0", "gz_1")

gamma_gas = 1.4
elem_width = 1.0
cfl_euler = 0.5
alpha_most = 0.5
indicator_level = 0.5 * 10.0 ** (-1.8 * 4.0**0.25)
indicator_slope = math.log((1.0 - 0.0001) / 0.0001) / indicator_level
coupling = 10.0
pseudo_step = 0.3 * elem_width / 7.0
rho_offset = 2.3

NX, NY, NZ = (4, 8, 128)
F32 = jnp.float32


def lgl_tables():
    points = np.array([-1.0, -1.0 / math.sqrt(5.0), 1.0 / math.sqrt(5.0), 1.0])
    weights = np.array([1.0, 5.0, 5.0, 1.0]) / 6.0
    barycentric = np.array(
        [1.0 / np.prod([points[a] - points[b] for b in range(4) if b != a]) for a in range(4)]
    )
    derivative = np.zeros((4, 4))
    for a in range(4):
        for b in range(4):
            if b != a:
                derivative[a, b] = barycentric[b] / barycentric[a] / (points[a] - points[b])
        derivative[a, a] = -np.sum(derivative[a])
    legendre = np.stack(
        [np.ones(4), points, 0.5 * (3.0 * points**2 - 1.0), 0.5 * (5.0 * points**3 - 3.0 * points)],
        axis=1,
    )
    legendre = legendre * np.sqrt((2.0 * np.arange(4) + 1.0) / 2.0)
    gram = np.sum(weights[:, None] * legendre * legendre, axis=0)
    modal_map = (legendre * weights[:, None]).T / gram[:, None]
    return (weights, derivative, modal_map)


WEIGHTS, DERIV, MODAL = lgl_tables()


class Line:
    def __init__(self, dim):
        self.dim = dim
        self.length = (NY, NZ)[dim]
        self.at = lax.broadcasted_iota(jnp.int32, (NY, NZ), dim)
        self.node = self.at % 4
        self.lowest = self.at == 0
        self.highest = self.at == self.length - 1
        self.is0 = self.node == 0
        self.is3 = self.node == 3

    def by_node(self, values):
        v = [float(item) for item in values]
        if v[1] == v[2] and v[0] == v[3]:
            return jnp.where(self.is0 | self.is3, v[0], v[1]).astype(F32)
        return jnp.where(
            self.node < 2,
            jnp.where(self.is0, v[0], v[1]),
            jnp.where(self.is3, v[3], v[2]),
        ).astype(F32)

    def roll(self, value, by):
        return pltpu.roll(value, by % self.length, self.dim)

    def cyc(self, value, k):
        return jnp.where(self.node < 4 - k, self.roll(value, -k), self.roll(value, 4 - k))

    def coef(self, matrix, k, scale=1.0):
        return self.by_node([scale * matrix[i, (i + k) % 4] for i in range(4)])

    def element_sum(self, value):
        value = value + self.cyc(value, 2)
        return value + self.cyc(value, 1)


def load(ref):
    return [[ref[c, x] for x in range(NX)] for c in range(ref.shape[0])]


def is_even():
    return [lax.axis_index(axis) % 2 == 0 for axis in ("gx_1", "gy", "gz_1")]


def pack_x(comps, other, pair):
    even = is_even()[0]
    for c, comp in enumerate(comps):
        other[c] = jnp.where(even, comp[0], comp[NX - 1])
        pair[c] = jnp.where(even, comp[NX - 1], comp[0])


def pack_y(comps, other, pair):
    even = is_even()[1]
    for c, comp in enumerate(comps):
        for x, tile in enumerate(comp):
            low, high = (tile[0:1, :], tile[NY - 1 : NY, :])
            other[c, pl.ds(x, 1), :] = jnp.where(even, low, high)
            pair[c, pl.ds(x, 1), :] = jnp.where(even, high, low)


def pack_z(tiles, other, pair):
    even = is_even()[2]
    lane = lax.broadcasted_iota(jnp.int32, (NY, NZ), 1)
    first = jnp.zeros((NY, NZ), F32)
    last = jnp.zeros((NY, NZ), F32)
    for k, tile in enumerate(tiles):
        here = lane == k
        first = jnp.where(here, pltpu.roll(tile, k, 1) if k else tile, first)
        last = jnp.where(here, pltpu.roll(tile, k + 1, 1), last)
    other[...] = jnp.where(even, first, last)
    pair[...] = jnp.where(even, last, first)


def flat(comps):
    return [tile for comp in comps for tile in comp]


class Halo:
    def __init__(self, refs):
        self.even = is_even()
        self.refs = refs
        zo, zp = (refs[1][...], refs[4][...])
        self.zlo = jnp.where(self.even[2], zo, zp)
        self.zhi = jnp.where(self.even[2], zp, zo)

    def x_low(self, c):
        return jnp.where(self.even[0], self.refs[0][c], self.refs[5][c])

    def x_high(self, c):
        return jnp.where(self.even[0], self.refs[5][c], self.refs[0][c])

    def row(self, c, x, pair, other):
        line = jnp.where(self.even[1], self.refs[pair][c, pl.ds(x, 1), :], self.refs[other][c, pl.ds(x, 1), :])
        return jnp.broadcast_to(line, (NY, NZ))

    def low(self, dim, c, x):
        if dim == 0:
            return self.row(c, x, 2, 3)
        k = c * NX + x
        return pltpu.roll(self.zlo, (NZ - k) % NZ, 1) if k else self.zlo

    def high(self, dim, c, x):
        if dim == 0:
            return self.row(c, x, 3, 2)
        k = c * NX + x
        return pltpu.roll(self.zhi, NZ - 1 - k, 1)


def log_mean(left, right):
    total = left + right
    gap = right - left
    slope = gap / total
    ratio_sq = slope * slope
    is_close = ratio_sq < 0.0001
    series = 2.0 + ratio_sq * (2.0 / 3.0 + ratio_sq * (2.0 / 5.0 + ratio_sq * (2.0 / 7.0)))
    top = jnp.where(is_close, total, gap)
    low = jnp.where(is_close, series, jnp.log(right / left))
    return top / low


def two_point(left, right, d):
    rho_mean = log_mean(left[0], right[0])
    inv_mean = left[4] * right[4] / log_mean(left[0] * right[4], right[0] * left[4])
    vel = [0.5 * (left[1 + i] + right[1 + i]) for i in range(3)]
    product = left[1] * right[1] + left[2] * right[2] + left[3] * right[3]
    mass = rho_mean * vel[d]
    flux = [mass] + [mass * vel[i] for i in range(3)]
    flux[1 + d] = flux[1 + d] + 0.5 * (left[4] + right[4])
    energy = mass * (0.5 * product + inv_mean * (1.0 / (gamma_gas - 1.0))) + 0.5 * (
        left[4] * right[1 + d] + right[4] * left[1 + d]
    )
    return flux + [energy]


def primitive(u):
    inv = 1.0 / u[0]
    vel = [u[1 + i] * inv for i in range(3)]
    kinetic = u[1] * vel[0] + u[2] * vel[1] + u[3] * vel[2]
    pressure = (gamma_gas - 1.0) * (u[4] - 0.5 * kinetic)
    return (vel, pressure, jnp.sqrt(gamma_gas * pressure * inv))


def face_data(u, d, known=None):
    vel, pressure, sound = known or primitive(u)
    normal = vel[d]
    flux = [u[1 + d]] + [u[1 + i] * normal for i in range(3)] + [(u[4] + pressure) * normal]
    flux[1 + d] = flux[1 + d] + pressure
    return (u, flux, jnp.abs(normal) + sound)


def interface(left, right):
    speed = jnp.maximum(left[2], right[2])
    return [
        0.5 * ((left[1][c] + right[1][c]) - speed * (right[0][c] - left[0][c])) for c in range(5)
    ]


def volume_kernel(u_ref, vol_ref, alpha_ref, fast_ref):
    y, z = (Line(0), Line(1))
    u = load(u_ref)
    known = [primitive([u[c][x] for c in range(5)]) for x in range(NX)]
    nodes = [[u[0][x]] + known[x][0] + [known[x][1]] for x in range(NX)]
    speed = [
        jnp.abs(known[x][0][0]) + jnp.abs(known[x][0][1]) + jnp.abs(known[x][0][2]) + 3.0 * known[x][2]
        for x in range(NX)
    ]
    fast_ref[...] = jnp.maximum(jnp.maximum(speed[0], speed[1]), jnp.maximum(speed[2], speed[3]))

    product = [u[0][x] * known[x][1] for x in range(NX)]
    coeffs = [sum(float(MODAL[a, i]) * product[i] for i in range(4)) for a in range(4)]
    for line in (y, z):
        modal = [line.coef(MODAL, k) for k in range(4)]
        coeffs = [
            modal[0] * value + sum(modal[k] * line.cyc(value, k) for k in range(1, 4))
            for value in coeffs
        ]
    energy = [value * value for value in coeffs]
    total = (energy[0] + energy[1]) + (energy[2] + energy[3])
    low = (energy[0] + energy[1]) + energy[2]
    high = energy[3] + jnp.where(y.is3 | z.is3, low, 0.0)
    share = z.element_sum(y.element_sum(high)) / z.element_sum(y.element_sum(total))
    alpha = alpha_most / (1.0 + jnp.exp(-indicator_slope * (share - indicator_level)))
    alpha_ref[...] = alpha

    volume = [[None] * NX for _ in range(5)]
    for i in range(NX):
        for j in range(i + 1, NX):
            flux = two_point(nodes[i], nodes[j], 0)
            for c in range(5):
                for at, other in ((i, j), (j, i)):
                    term = (2.0 * DERIV[at, other]).astype(np.float32) * flux[c]
                    volume[c][at] = term if volume[c][at] is None else volume[c][at] + term
    for d, line in ((1, y), (2, z)):
        up, across, down = [line.coef(DERIV, k, 2.0) for k in (1, 2, 3)]
        for x in range(NX):
            near = two_point(nodes[x], [line.cyc(a, 1) for a in nodes[x]], d)
            far = two_point(nodes[x], [line.cyc(a, 2) for a in nodes[x]], d)
            for c in range(5):
                volume[c][x] = volume[c][x] + (
                    up * near[c] + down * line.cyc(near[c], 3) + across * far[c]
                )
    keep = 1.0 - alpha
    for c in range(5):
        for x in range(NX):
            vol_ref[c, x] = keep * volume[c][x]


def gravity_parts(field, halo, base, y, z):
    total = [[0.0] * NX for _ in range(4)]
    have = [c for c in range(4) if field[c] is not None]
    where = {c: base + i for i, c in enumerate(have)}

    for c, partner in ((0, 1), (1, 0)):
        if field[partner] is not None:
            for i in range(NX):
                terms = [float(2.0 * DERIV[i, j]) * field[partner][j] for j in range(NX) if DERIV[i, j] != 0.0]
                total[c][i] = total[c][i] + sum(terms[1:], terms[0])
    jumps = {}
    for c in have if halo is not None else ():
        jumps[c] = (halo.x_low(where[c]) - field[c][0], halo.x_high(where[c]) - field[c][NX - 1])
        for side, x in ((0, 0), (1, NX - 1)):
            total[c][x] = total[c][x] + 6.0 * jumps[c][side]
    for c, partner in ((0, 1), (1, 0)):
        if partner in jumps:
            total[c][0] = total[c][0] - 6.0 * jumps[partner][0]
            total[c][NX - 1] = total[c][NX - 1] + 6.0 * jumps[partner][1]
    for d, line in ((1, y), (2, z)):
        comp = 1 + d
        diag = line.coef(DERIV, 0, 2.0)
        coefs = [line.coef(DERIV, k, 2.0) for k in range(1, 4)]
        sign = line.by_node([-6.0, 0.0, 0.0, 6.0])
        for x in range(NX):
            for c, partner in ((0, comp), (comp, 0)):
                if field[partner] is not None:
                    value = field[partner][x]
                    term = diag * value
                    for k in range(1, 4):
                        term = term + coefs[k - 1] * line.cyc(value, k)
                    total[c][x] = total[c][x] + term
            gaps = {}
            for c in have:
                value = field[c][x]
                low, high = (value, value)
                if halo is not None:
                    low = halo.low(line.dim, where[c], x)
                    high = halo.high(line.dim, where[c], x)
                prev = jnp.where(line.lowest, low, line.roll(value, 1))
                after = jnp.where(line.highest, high, line.roll(value, -1))
                beside = jnp.where(line.is0, prev, jnp.where(line.is3, after, value))
                gaps[c] = beside - value
                total[c][x] = total[c][x] + 6.0 * gaps[c]
            for c, partner in ((0, comp), (comp, 0)):
                if partner in gaps:
                    total[c][x] = total[c][x] + sign * gaps[partner]
    return total


def advance(field, halo, base, y, z, source):
    total = gravity_parts(field, halo, base, y, z)
    phi_rate = [total[0][x] - coupling * source[x] for x in range(NX)]
    new = [[None] * NX for _ in range(4)]
    for x in range(NX):
        change = pseudo_step * phi_rate[x]
        new[0][x] = change if field[0] is None else field[0][x] + change
        for c in range(1, 4):
            if field[c] is None:
                new[c][x] = pseudo_step * total[c][x]
            else:
                new[c][x] = field[c][x] + pseudo_step * (total[c][x] - field[c][x])
    return (new, phi_rate)


def pack_kernel(u_ref, g_ref, u_out, g_out, *outs):
    u_out[...] = u_ref[...]
    g_out[...] = g_ref[...]
    comps = load(u_ref) + load(g_ref)
    xo, zo, yo, yp, zp, xp = outs
    pack_x(comps, xo, xp)
    pack_y(comps, yo, yp)
    pack_z(flat(comps), zo, zp)


def face_kernel(u_ref, g_ref, vol_ref, alpha_ref, *refs):
    halo = Halo(refs[:6])
    rate_ref, f1_ref, f2_ref, xo, yo, yp, xp = refs[6:]
    y, z = (Line(0), Line(1))
    u = load(u_ref)
    g = load(g_ref)
    alpha = alpha_ref[...]
    keep = 1.0 - alpha
    known = [primitive([u[c][x] for c in range(5)]) for x in range(NX)]
    total = load(vol_ref)

    own = [face_data([u[c][x] for c in range(5)], 0, known[x]) for x in range(NX)]
    below = face_data([halo.x_low(c) for c in range(5)], 0)
    above = face_data([halo.x_high(c) for c in range(5)], 0)
    chain = [below] + own + [above]
    faces = [interface(chain[i], chain[i + 1]) for i in range(NX + 1)]
    for x in range(NX):
        inner = alpha * float(1.0 / WEIGHTS[x])
        edge = inner + keep * 6.0
        low_coef = edge if x == 0 else inner
        high_coef = edge if x == NX - 1 else inner
        for c in range(5):
            total[c][x] = total[c][x] + (high_coef * faces[x + 1][c] - low_coef * faces[x][c])
    for d, line in ((1, y), (2, z)):
        inner = alpha * line.by_node(1.0 / WEIGHTS)
        low_coef = inner + keep * line.by_node([6.0, 0.0, 0.0, 0.0])
        high_coef = inner + keep * line.by_node([0.0, 0.0, 0.0, 6.0])
        for x in range(NX):
            mine = face_data([u[c][x] for c in range(5)], d, known[x])
            prev = face_data(
                [
                    jnp.where(line.lowest, halo.low(line.dim, c, x), line.roll(u[c][x], 1))
                    for c in range(5)
                ],
                d,
            )
            after = face_data(
                [jnp.where(line.highest, halo.high(line.dim, c, x), u[c][x]) for c in range(5)], d
            )
            face = interface(prev, mine)
            end = interface(mine, after)
            for c in range(5):
                following = jnp.where(line.highest, end[c], line.roll(face[c], -1))
                total[c][x] = total[c][x] + (high_coef * following - low_coef * face[c])
    rate = [[-2.0 * total[c][x] for x in range(NX)] for c in range(5)]
    for x in range(NX):
        for i in range(3):
            rate[1 + i][x] = rate[1 + i][x] - u[0][x] * g[1 + i][x]
        rate[4][x] = rate[4][x] - (
            u[1][x] * g[1][x] + u[2][x] * g[2][x] + u[3][x] * g[3][x]
        )
        for c in range(5):
            rate_ref[c, x] = rate[c][x]

    source = [u[0][x] - rho_offset for x in range(NX)]
    new, _ = advance(g, halo, 5, y, z, source)
    slope = [(-pseudo_step * coupling) * rate[0][x] for x in range(NX)]
    partial, _ = advance(new, None, 0, y, z, source)
    partial_slope, _ = advance([slope, None, None, None], None, 0, y, z, rate[0])
    f1 = new + [slope]
    f2 = partial + partial_slope
    for x in range(NX):
        for c in range(5):
            f1_ref[c, x] = f1[c][x]
        for c in range(8):
            f2_ref[c, x] = f2[c][x]
    pack_x(f1 + f2, xo, xp)
    pack_y(f1 + f2, yo, yp)


def face_terms(gap, d, sign):
    terms = [None if value is None else 6.0 * value for value in gap]
    for c, partner in ((0, 1 + d), (1 + d, 0)):
        if gap[partner] is not None:
            extra = sign * gap[partner]
            terms[c] = extra if terms[c] is None else terms[c] + extra
    return terms


def meet(field, gap, d, sign):
    terms = face_terms(gap[:4], d, sign) + face_terms([gap[4], None, None, None], d, sign)
    return [
        value if term is None else value + pseudo_step * term for value, term in zip(field, terms)
    ]


def ends(line):
    outer = line.lowest | line.highest
    sign = jnp.where(line.lowest, -6.0, jnp.where(line.highest, 6.0, 0.0)).astype(F32)
    return (outer, sign)


def at(field, x, first, count):
    return [field[first + c][x] for c in range(count)]


def join_kernel(f1_ref, f2_ref, xo, yo, yp, xp, f2_out, side_ref, row_ref, zo, zp, eo, ep):
    even = is_even()
    y = Line(0)
    f1, f2 = (load(f1_ref), load(f2_ref))
    sides = []
    for low, x, sign in ((True, 0, -6.0), (False, NX - 1, 6.0)):
        near, away = (xo, xp) if low else (xp, xo)
        side = [jnp.where(even[0], near[c], away[c]) for c in range(13)]
        gap = [side[c] - f1[c][x] for c in range(5)]
        for c, value in enumerate(meet(at(f2, x, 0, 8), gap, 0, sign)):
            f2[c][x] = value
        side[5:] = meet(side[5:], [-value for value in gap], 0, -sign)
        sides.append(side)
    outer, sign = ends(y)
    rows = [[None] * NX for _ in range(13)]
    for x in range(NX):
        for c in range(13):
            other, pair = (yo[c, pl.ds(x, 1), :], yp[c, pl.ds(x, 1), :])
            low = jnp.broadcast_to(jnp.where(even[1], other, pair), (NY, NZ))
            high = jnp.broadcast_to(jnp.where(even[1], pair, other), (NY, NZ))
            rows[c][x] = jnp.where(y.lowest, low, jnp.where(y.highest, high, 0.0))
        gap = [jnp.where(outer, rows[c][x] - f1[c][x], 0.0) for c in range(5)]
        for c, value in enumerate(meet(at(f2, x, 0, 8), gap, 1, sign)):
            f2[c][x] = value
        for c, value in enumerate(meet(at(rows, x, 5, 8), [-v for v in gap], 1, -sign)):
            rows[5 + c][x] = value
    for x in range(NX):
        for c in range(8):
            f2_out[c, x] = f2[c][x]
        for c in range(13):
            row_ref[c, x] = rows[c][x]
    for w, side in enumerate(sides):
        for c in range(13):
            side_ref[w, c] = side[c]
        for c in range(5):
            low, high = (side[c][0:1, :], side[c][NY - 1 : NY, :])
            eo[pl.ds(5 * w + c, 1), :] = jnp.where(even[1], low, high)
            ep[pl.ds(5 * w + c, 1), :] = jnp.where(even[1], high, low)
    pack_z(flat(f1 + f2) + sides[0][:5] + sides[1][:5] + flat(rows[:5]), zo, zp)


class Around:
    def __init__(self, sides, rows, columns):
        self.sides, self.rows, self.columns = (sides, rows, columns)

    def x_low(self, c):
        return self.sides[0][c]

    def x_high(self, c):
        return self.sides[1][c]

    def low(self, dim, c, x):
        return (self.rows, self.columns)[dim][c][x]

    high = low


def last_kernel(
    u_ref, rate_ref, fast_ref, f1_ref, f2_ref, side_ref, row_ref, zo, zp, eo, ep, next_ref, stat_ref
):
    even = is_even()
    y, z = (Line(0), Line(1))
    f1, f2, rows = (load(f1_ref), load(f2_ref), load(row_ref))
    sides = [[side_ref[w, c] for c in range(13)] for w in range(2)]
    z_other, z_pair = (zo[...], zp[...])
    z_low = jnp.where(even[2], z_other, z_pair)
    z_high = jnp.where(even[2], z_pair, z_other)
    z_outer, z_sign = ends(z)
    y_outer, y_sign = ends(y)

    def column(k):
        low = pltpu.roll(z_low, (NZ - k) % NZ, 1) if k else z_low
        return jnp.where(z.lowest, low, pltpu.roll(z_high, NZ - 1 - k, 1))

    def gaps(outer, beside, own):
        return [jnp.where(outer, b - o, 0.0) for b, o in zip(beside, own)]

    columns = [[column(c * NX + x) for x in range(NX)] for c in range(13)]
    for x in range(NX):
        gap = gaps(z_outer, at(columns, x, 0, 5), at(f1, x, 0, 5))
        for c, value in enumerate(meet(at(f2, x, 0, 8), gap, 2, z_sign)):
            f2[c][x] = value
        for c, value in enumerate(meet(at(columns, x, 5, 8), [-v for v in gap], 2, -z_sign)):
            columns[5 + c][x] = value
    for w, x, sign in ((0, 0, -6.0), (1, NX - 1, 6.0)):
        corner = []
        for c in range(5):
            other, pair = (eo[pl.ds(5 * w + c, 1), :], ep[pl.ds(5 * w + c, 1), :])
            low = jnp.broadcast_to(jnp.where(even[1], other, pair), (NY, NZ))
            high = jnp.broadcast_to(jnp.where(even[1], pair, other), (NY, NZ))
            corner.append(jnp.where(y.lowest, low, high))
        side = sides[w]
        beside = [column(13 * NX + 5 * w + c) for c in range(5)]
        side[5:] = meet(side[5:], gaps(z_outer, beside, side[:5]), 2, z_sign)
        side[5:] = meet(side[5:], gaps(y_outer, corner, side[:5]), 1, y_sign)
        gap = gaps(y_outer, corner, at(rows, x, 0, 5))
        for c, value in enumerate(meet(at(rows, x, 5, 8), gap, 0, sign)):
            rows[5 + c][x] = value
    for x in range(NX):
        beside = [column(13 * NX + 10 + c * NX + x) for c in range(5)]
        gap = gaps(z_outer & y_outer, beside, at(rows, x, 0, 5))
        for c, value in enumerate(meet(at(rows, x, 5, 8), gap, 2, z_sign)):
            rows[5 + c][x] = value

    around = Around([side[5:] for side in sides], rows[5:], columns[5:])
    source = [u_ref[0, x] - rho_offset for x in range(NX)]
    new, base_rate = advance(f2[:4], around, 0, y, z, source)
    slope, slope_rate = advance(f2[4:], around, 4, y, z, [rate_ref[0, x] for x in range(NX)])
    comps = new + slope
    for c in range(8):
        for x in range(NX):
            next_ref[c, x] = comps[c][x]
    weight = y.by_node(WEIGHTS) * z.by_node(WEIGHTS)

    def total(values):
        by_x = [float(WEIGHTS[x]) * values[x] for x in range(NX)]
        return jnp.sum(((by_x[0] + by_x[1]) + (by_x[2] + by_x[3])) * weight)

    stats = [
        jnp.max(fast_ref[...]),
        total([a * a for a in base_rate]),
        total([a * b for a, b in zip(base_rate, slope_rate)]),
        total([b * b for b in slope_rate]),
        total(base_rate),
        total(slope_rate),
        total(source),
    ]
    lane = lax.broadcasted_iota(jnp.int32, (1, NZ), 1)
    out = jnp.zeros((1, NZ), F32)
    for i, value in enumerate(stats):
        out = jnp.where(lane == i, value, out)
    stat_ref[...] = out


def finish_kernel(weight_total, u_ref, rate_ref, field_ref, stat_ref, grav_ref, source_ref, norm_ref):
    stat = stat_ref[...]
    part = [stat[:, i : i + 1] for i in range(7)]
    step = cfl_euler * elem_width / (7.0 * part[0])
    mean = part[6] * (1.0 / weight_total)
    shift = coupling * mean
    squares = (
        part[1]
        + step * (2.0 * part[2] + step * part[3])
        + shift * (2.0 * (part[4] + step * part[5]) + shift * weight_total)
    )
    norm_ref[...] = jnp.sqrt(jnp.maximum(squares, 0.0) * (1.0 / weight_total))
    raised = (ITERS * pseudo_step) * shift
    for x in range(NX):
        phi = field_ref[0, x] + step * field_ref[4, x] + raised
        grad = [field_ref[c, x] + step * field_ref[4 + c, x] for c in range(1, 4)]
        grav_ref[0, x] = phi
        for c in range(3):
            grav_ref[1 + c, x] = grad[c]
        rho = u_ref[0, x] + step * rate_ref[0, x]
        work = 0.0
        for c in range(3):
            source_ref[c, x] = -rho * grad[c]
            work = work + (u_ref[1 + c, x] + step * rate_ref[1 + c, x]) * grad[c]
        source_ref[3, x] = -work


def call(kernel, out_shape, flops, on_chip=True):
    def run(*args):
        if on_chip:
            args = [pltpu.with_memory_space_constraint(a, pltpu.VMEM) for a in args]
        return pl.pallas_call(
            kernel,
            in_specs=[pl.BlockSpec(memory_space=pltpu.VMEM)] * len(args),
            out_specs=[pl.BlockSpec(memory_space=pltpu.VMEM)] * len(out_shape),
            out_shape=out_shape,
            cost_estimate=pl.CostEstimate(flops=flops, bytes_accessed=400000, transcendentals=0),
        )(*args)

    return run


def pair_of(i, size):
    return i ^ 1


def other_of(i, size):
    return (i + 1 if i % 2 else i - 1) % size


ROUTES = {
    "state": (
        (GX, other_of),
        (GZ, other_of),
        ("gy", other_of),
        ("gy", pair_of),
        (GZ, pair_of),
        (GX, pair_of),
    ),
    "second": ((GX, other_of), ("gy", other_of), ("gy", pair_of), (GX, pair_of)),
    "third": ((GZ, other_of), (GZ, pair_of), ("gy", other_of), ("gy", pair_of)),
}


def exchange(messages, stage):
    received = []
    for message, (axis, partner) in zip(messages, ROUTES[stage]):
        size = lax.axis_size(axis)
        received.append(lax.ppermute(message, axis, [(a, partner(a, size)) for a in range(size)]))
    return received


def gather(stat, axis):
    lane = lax.broadcasted_iota(jnp.int32, (1, NZ), 1)
    every = lax.all_gather(stat, axis, tiled=True)
    return jnp.where(
        lane == 0, jnp.max(every, axis=0, keepdims=True), jnp.sum(every, axis=0, keepdims=True)
    )


def spread(stat):
    names = ("gx_0", "gx_1", "gy", "gz_0", "gz_1")
    sizes = [lax.axis_size(name) for name in names]
    ring = sizes[0] * sizes[3]
    pairs = []
    for at in np.ndindex(*sizes):
        a, core, b, c, e = at
        place = (a * sizes[3] + c + core * sizes[4] + e - (sizes[3] // 2 - 1)) % ring
        to = (place // sizes[3], core, b, place % sizes[3], e)
        pairs.append(
            (int(np.ravel_multi_index(at, sizes)), int(np.ravel_multi_index(to, sizes)))
        )
    return lax.ppermute(stat, names, pairs)


def over_all(stat):
    for axis in ("gx_1", "gy", "gz_1"):
        stat = gather(stat, axis)
    stat = spread(stat)
    for axis in ("gx_1", "gz_1", "gx_0"):
        stat = gather(stat, axis)
    return stat


def shape(*dims):
    return pltpu.VMEM(dims, F32)


def local(u, g):
    weight_total = float(
        8.0
        * (u.shape[1] // 4 * lax.axis_size(GX))
        * (u.shape[2] // 4 * lax.axis_size("gy"))
        * (u.shape[3] // 4 * lax.axis_size(GZ))
    )
    full = (NX, NY, NZ)
    tile = shape(NY, NZ)
    planes, rows = (shape(9, NY, NZ), shape(9, NX, NZ))
    u, g, *messages = call(
        pack_kernel,
        [shape(5, *full), shape(4, *full), planes, tile, rows, rows, tile, planes],
        10**5,
        False,
    )(u, g)
    received = exchange(messages, "state")
    vol, alpha, fast = call(volume_kernel, [shape(5, *full), tile, tile], 10**7)(u)
    planes, rows = (shape(13, NY, NZ), shape(13, NX, NZ))
    rate, f1, f2, *messages = call(
        face_kernel,
        [shape(5, *full), shape(5, *full), shape(8, *full), planes, rows, rows, planes],
        10**6,
    )(u, g, vol, alpha, *received)
    received = exchange(messages, "second")
    corners = shape(10, NZ)
    f2, sides, rows, *messages = call(
        join_kernel,
        [shape(8, *full), shape(2, 13, NY, NZ), shape(13, *full), tile, tile, corners, corners],
        10**6,
    )(f1, f2, *received)
    received = exchange(messages, "third")
    field, stat = call(last_kernel, [shape(8, *full), shape(1, NZ)], 10**6)(
        u, rate, fast, f1, f2, sides, rows, *received
    )
    stat = over_all(stat)
    gravity, gravity_source, norm = call(
        functools.partial(finish_kernel, weight_total),
        [jax.ShapeDtypeStruct((4, *full), F32)] * 2 + [jax.ShapeDtypeStruct((1, 1), F32)],
        10**5,
    )(u, rate, field, stat)
    return (rate, gravity, gravity_source, norm.reshape(()))


def solution(mesh):
    torus = Mesh(
        mesh.devices.reshape(4, 2, mesh.shape["gy"], 8, 4), ("gx_0", "gx_1", "gy", "gz_0", "gz_1")
    )
    placed = (P(None, GX, "gy", GZ), P(None, GX, "gy", GZ))
    return jax.shard_map(
        local,
        mesh=torus,
        in_specs=placed,
        out_specs=(P(None, GX, "gy", GZ), P(None, GX, "gy", GZ), P(None, GX, "gy", GZ), P()),
        check_vma=False,
    )
```

profile of v0, /device:TPU:72, one launch (start us, length us, event | category | flops | bytes accessed | tf_op | source)
XLA Modules:
  0.0 148.4 jit_solution(6061037984366991440)
XLA Ops:
  0.6 1.0 shard_map.57
  1.7 20.6 %collective-permute-start = (f32[9,8,128]{2,1,0:T(8,128)S(1)}, f32[9,8,128]{2,1,0:T(8,128)S(1)}, u32[]{:S(2)}, u32[]{:S(2)}) collective-permute-start(f32[9,8,128]{2,1,0:T(8,128)S(1)} %get-tuple-element.38), channel_id=1, source_target_pairs={{0,896},{128,256},{256,128},{384,512},{512,384},{640,768},{768,640... | collective-permute-start | bytes 110600 | tf_op jit(solution)/shard_map/ppermute | solution.py:636
  22.3 1.9 %collective-permute-start.5 = (f32[9,8,128]{2,1,0:T(8,128)S(1)}, f32[9,8,128]{2,1,0:T(8,128)S(1)}, u32[]{:S(2)}, u32[]{:S(2)}) collective-permute-start(f32[9,8,128]{2,1,0:T(8,128)S(1)} %get-tuple-element.43), channel_id=1, source_target_pairs={{0,128},{128,0},{256,384},{384,256},{512,640},{640,512},{768,896},... | collective-permute-start | bytes 110600 | tf_op jit(solution)/shard_map/ppermute | solution.py:636
  24.2 4.7 %collective-permute-start.2 = (f32[9,4,128]{2,1,0:T(4,128)S(1)}, f32[9,4,128]{2,1,0:T(4,128)S(1)}, u32[]{:S(2)}, u32[]{:S(2)}) collective-permute-start(f32[9,4,128]{2,1,0:T(4,128)S(1)} %get-tuple-element.40), channel_id=1, source_target_pairs={{0,96},{32,64},{64,32},{96,0},{1,97},{33,65},{65,33},{97,1},{2,98}... | collective-permute-start | bytes 55304 | tf_op jit(solution)/shard_map/ppermute | solution.py:636
  28.9 2.1 %collective-permute-start.3 = (f32[9,4,128]{2,1,0:T(4,128)S(1)}, f32[9,4,128]{2,1,0:T(4,128)S(1)}, u32[]{:S(2)}, u32[]{:S(2)}) collective-permute-start(f32[9,4,128]{2,1,0:T(4,128)S(1)} %get-tuple-element.41), channel_id=1, source_target_pairs={{0,32},{32,0},{64,96},{96,64},{1,33},{33,1},{65,97},{97,65},{2,34}... | collective-permute-start | bytes 55304 | tf_op jit(solution)/shard_map/ppermute | solution.py:636
  31.1 3.5 %collective-permute-start.1 = (f32[8,128]{1,0:T(8,128)S(1)}, f32[8,128]{1,0:T(8,128)S(1)}, u32[]{:S(2)}, u32[]{:S(2)}) collective-permute-start(f32[8,128]{1,0:T(8,128)S(1)} %get-tuple-element.39), channel_id=1, source_target_pairs={{0,31},{1,2},{2,1},{3,4},{4,3},{5,6},{6,5},{7,8},{8,7},{9,10},{10,... | collective-permute-start | bytes 12296 | tf_op jit(solution)/shard_map/ppermute | solution.py:636
  34.6 2.0 %collective-permute-done.1.refs_1_ = f32[8,128]{1,0:T(8,128)S(1)} collective-permute-done((f32[8,128]{1,0:T(8,128)S(1)}, f32[8,128]{1,0:T(8,128)S(1)}, u32[]{:S(2)}, u32[]{:S(2)}) %collective-permute-start.1) | collective-permute-done | bytes 4128 | tf_op jit(solution)/shard_map/ppermute | solution.py:636
  36.6 4.5 %collective-permute-start.4 = (f32[8,128]{1,0:T(8,128)S(1)}, f32[8,128]{1,0:T(8,128)S(1)}, u32[]{:S(2)}, u32[]{:S(2)}) collective-permute-start(f32[8,128]{1,0:T(8,128)S(1)} %get-tuple-element.42), channel_id=1, source_target_pairs={{0,1},{1,0},{2,3},{3,2},{4,5},{5,4},{6,7},{7,6},{8,9},{9,8},{10,11... | collective-permute-start | bytes 12296 | tf_op jit(solution)/shard_map/ppermute | solution.py:636
  41.0 0.4 shard_map.58
  41.5 1.1 collective-permute-done.4.refs_4_
  42.6 0.0 collective-permute-done.2.refs_2_
  42.6 0.0 collective-permute-done.3.refs_3_
  42.6 0.0 collective-permute-done.refs_0_
  42.6 0.0 collective-permute-done.5.refs_5_
  42.6 0.6 shard_map.59
  43.2 6.0 %collective-permute-start.6 = (f32[13,8,128]{2,1,0:T(8,128)S(1)}, f32[13,8,128]{2,1,0:T(8,128)S(1)}, u32[]{:S(2)}, u32[]{:S(2)}) collective-permute-start(f32[13,8,128]{2,1,0:T(8,128)S(1)} %get-tuple-element.48), channel_id=1, source_target_pairs={{0,896},{128,256},{256,128},{384,512},{512,384},{640,768},{768,640... | collective-permute-start | bytes 159752 | tf_op jit(solution)/shard_map/ppermute | solution.py:636
  49.2 5.1 %collective-permute-start.9 = (f32[13,8,128]{2,1,0:T(8,128)S(1)}, f32[13,8,128]{2,1,0:T(8,128)S(1)}, u32[]{:S(2)}, u32[]{:S(2)}) collective-permute-start(f32[13,8,128]{2,1,0:T(8,128)S(1)} %get-tuple-element.51), channel_id=1, source_target_pairs={{0,128},{128,0},{256,384},{384,256},{512,640},{640,512},{768,896},... | collective-permute-start | bytes 159752 | tf_op jit(solution)/shard_map/ppermute | solution.py:636
  54.4 3.0 %collective-permute-start.7 = (f32[13,4,128]{2,1,0:T(4,128)S(1)}, f32[13,4,128]{2,1,0:T(4,128)S(1)}, u32[]{:S(2)}, u32[]{:S(2)}) collective-permute-start(f32[13,4,128]{2,1,0:T(4,128)S(1)} %get-tuple-element.49), channel_id=1, source_target_pairs={{0,96},{32,64},{64,32},{96,0},{1,97},{33,65},{65,33},{97,1},{2,98}... | collective-permute-start | bytes 79880 | tf_op jit(solution)/shard_map/ppermute | solution.py:636
  57.4 2.6 %collective-permute-start.8 = (f32[13,4,128]{2,1,0:T(4,128)S(1)}, f32[13,4,128]{2,1,0:T(4,128)S(1)}, u32[]{:S(2)}, u32[]{:S(2)}) collective-permute-start(f32[13,4,128]{2,1,0:T(4,128)S(1)} %get-tuple-element.50), channel_id=1, source_target_pairs={{0,32},{32,0},{64,96},{96,64},{1,33},{33,1},{65,97},{97,65},{2,34}... | collective-permute-start | bytes 79880 | tf_op jit(solution)/shard_map/ppermute | solution.py:636
  60.0 1.3 collective-permute-done.7.yo
  61.3 1.8 %collective-permute-done.8.yp = f32[13,4,128]{2,1,0:T(4,128)S(1)} collective-permute-done((f32[13,4,128]{2,1,0:T(4,128)S(1)}, f32[13,4,128]{2,1,0:T(4,128)S(1)}, u32[]{:S(2)}, u32[]{:S(2)}) %collective-permute-start.8) | collective-permute-done | bytes 26656 | tf_op jit(solution)/shard_map/ppermute | solution.py:636
  63.2 0.0 collective-permute-done.6.xo
  63.2 0.0 collective-permute-done.9.xp
  63.2 0.3 shard_map.60
  63.4 4.0 %collective-permute-start.12 = (f32[10,128]{1,0:T(8,128)S(1)}, f32[10,128]{1,0:T(8,128)S(1)}, u32[]{:S(2)}, u32[]{:S(2)}) collective-permute-start(f32[10,128]{1,0:T(8,128)S(1)} %get-tuple-element.57), channel_id=1, source_target_pairs={{0,96},{32,64},{64,32},{96,0},{1,97},{33,65},{65,33},{97,1},{2,98}... | collective-permute-start | bytes 15368 | tf_op jit(solution)/shard_map/ppermute | solution.py:636
  67.5 2.5 %collective-permute-start.13 = (f32[10,128]{1,0:T(8,128)S(1)}, f32[10,128]{1,0:T(8,128)S(1)}, u32[]{:S(2)}, u32[]{:S(2)}) collective-permute-start(f32[10,128]{1,0:T(8,128)S(1)} %get-tuple-element.58), channel_id=1, source_target_pairs={{0,32},{32,0},{64,96},{96,64},{1,33},{33,1},{65,97},{97,65},{2,34}... | collective-permute-start | bytes 15368 | tf_op jit(solution)/shard_map/ppermute | solution.py:636
  70.0 4.3 %collective-permute-start.10 = (f32[8,128]{1,0:T(8,128)S(1)}, f32[8,128]{1,0:T(8,128)S(1)}, u32[]{:S(2)}, u32[]{:S(2)}) collective-permute-start(f32[8,128]{1,0:T(8,128)S(1)} %get-tuple-element.55), channel_id=1, source_target_pairs={{0,31},{1,2},{2,1},{3,4},{4,3},{5,6},{6,5},{7,8},{8,7},{9,10},{10,... | collective-permute-start | bytes 12296 | tf_op jit(solution)/shard_map/ppermute | solution.py:636
  74.3 5.0 %collective-permute-start.11 = (f32[8,128]{1,0:T(8,128)S(1)}, f32[8,128]{1,0:T(8,128)S(1)}, u32[]{:S(2)}, u32[]{:S(2)}) collective-permute-start(f32[8,128]{1,0:T(8,128)S(1)} %get-tuple-element.56), channel_id=1, source_target_pairs={{0,1},{1,0},{2,3},{3,2},{4,5},{5,4},{6,7},{7,6},{8,9},{9,8},{10,11... | collective-permute-start | bytes 12296 | tf_op jit(solution)/shard_map/ppermute | solution.py:636
  79.3 0.0 collective-permute-done.10.zo
  79.3 1.6 %collective-permute-done.11.zp = f32[8,128]{1,0:T(8,128)S(1)} collective-permute-done((f32[8,128]{1,0:T(8,128)S(1)}, f32[8,128]{1,0:T(8,128)S(1)}, u32[]{:S(2)}, u32[]{:S(2)}) %collective-permute-start.11) | collective-permute-done | bytes 4128 | tf_op jit(solution)/shard_map/ppermute | solution.py:636
  80.8 0.0 collective-permute-done.12.eo
  80.8 0.0 collective-permute-done.13.ep
  80.8 0.5 shard_map.61
  81.4 1.8 %all-gather = f32[2,1,128]{2,1,0:T(1,128)S(1)} all-gather(f32[1,1,128]{2,1,0:T(1,128)S(1)} %bitcast.43), channel_id=1, replica_groups=mesh['gx_0'=4,'gx_1'=2,'gy'=4,'gz_0'=8,'gz_1'=4] {'gx_1'}, dimensions={0}, use_global_device_ids=true | all-gather | bytes 1536 | tf_op jit(solution)/shard_map/all_gather | solution.py:642
  83.2 8.4 %all-gather.1 = f32[4,1,128]{2,1,0:T(1,128)S(1)} all-gather(f32[1,1,128]{2,1,0:T(1,128)S(1)} %fusion.3), channel_id=1, replica_groups=mesh['gx_0'=4,'gx_1'=2,'gy'=4,'gz_0'=8,'gz_1'=4] {'gy'}, dimensions={0}, use_global_device_ids=true | all-gather | bytes 2560 | tf_op jit(solution)/shard_map/all_gather | solution.py:642
  91.6 9.0 %all-gather.2 = f32[4,1,128]{2,1,0:T(1,128)S(1)} all-gather(f32[1,1,128]{2,1,0:T(1,128)S(1)} %fusion.2), channel_id=1, replica_groups=mesh['gx_0'=4,'gx_1'=2,'gy'=4,'gz_0'=8,'gz_1'=4] {'gz_1'}, dimensions={0}, use_global_device_ids=true | all-gather | bytes 2560 | tf_op jit(solution)/shard_map/all_gather | solution.py:642
  100.6 13.3 %collective-permute-start.14 = (f32[1,128]{1,0:T(1,128)S(1)}, f32[1,128]{1,0:T(1,128)S(1)}, u32[]{:S(2)}, u32[]{:S(2)}) collective-permute-start(f32[1,128]{1,0:T(1,128)S(1)} %bitcast_select_fusion.3), channel_id=1, source_target_pairs={{0,788},{1,793},{2,798},{3,3},{4,792},{5,797},{6,2},{7,7},{8,796},... | collective-permute-start | bytes 1544 | tf_op jit(solution)/shard_map/ppermute | solution.py:660
  114.0 0.6 copy.6
  114.6 0.6 collective-permute-done.14
  115.2 1.8 %all-gather.3 = f32[2,1,128]{2,1,0:T(1,128)S(1)} all-gather(f32[1,1,128]{2,1,0:T(1,128)S(1)} %bitcast.44), channel_id=1, replica_groups=mesh['gx_0'=4,'gx_1'=2,'gy'=4,'gz_0'=8,'gz_1'=4] {'gx_1'}, dimensions={0}, use_global_device_ids=true | all-gather | bytes 1536 | tf_op jit(solution)/shard_map/all_gather | solution.py:642
  117.1 9.5 %all-gather.4 = f32[4,1,128]{2,1,0:T(1,128)S(1)} all-gather(f32[1,1,128]{2,1,0:T(1,128)S(1)} %fusion.1), channel_id=1, replica_groups=mesh['gx_0'=4,'gx_1'=2,'gy'=4,'gz_0'=8,'gz_1'=4] {'gz_1'}, dimensions={0}, use_global_device_ids=true | all-gather | bytes 2560 | tf_op jit(solution)/shard_map/all_gather | solution.py:642
  126.6 20.8 %all-gather.5 = f32[4,1,128]{2,1,0:T(1,128)S(1)} all-gather(f32[1,1,128]{2,1,0:T(1,128)S(1)} %fusion), channel_id=1, replica_groups=mesh['gx_0'=4,'gx_1'=2,'gy'=4,'gz_0'=8,'gz_1'=4] {'gx_0'}, dimensions={0}, use_global_device_ids=true | all-gather | bytes 2560 | tf_op jit(solution)/shard_map/all_gather | solution.py:642
  147.4 0.9 shard_map.62
  (12 shorter events, 0.2 us)
Async XLA Ops:
  1.7 40.9 %collective-permute-start = (f32[9,8,128]{2,1,0:T(8,128)S(1)}, f32[9,8,128]{2,1,0:T(8,128)S(1)}, u32[]{:S(2)}, u32[]{:S(2)}) collective-permute-start(f32[9,8,128]{2,1,0:T(8,128)S(1)} %get-tuple-element.38), channel_id=1, source_target_pairs={{0,896},{128,256},{256,128},{384,512},{512,384},{640,768},{768,640... | collective-permute-start | bytes 110600 | tf_op jit(solution)/shard_map/ppermute | solution.py:636
  22.3 20.3 %collective-permute-start.5 = (f32[9,8,128]{2,1,0:T(8,128)S(1)}, f32[9,8,128]{2,1,0:T(8,128)S(1)}, u32[]{:S(2)}, u32[]{:S(2)}) collective-permute-start(f32[9,8,128]{2,1,0:T(8,128)S(1)} %get-tuple-element.43), channel_id=1, source_target_pairs={{0,128},{128,0},{256,384},{384,256},{512,640},{640,512},{768,896},... | collective-permute-start | bytes 110600 | tf_op jit(solution)/shard_map/ppermute | solution.py:636
  24.2 18.4 %collective-permute-start.2 = (f32[9,4,128]{2,1,0:T(4,128)S(1)}, f32[9,4,128]{2,1,0:T(4,128)S(1)}, u32[]{:S(2)}, u32[]{:S(2)}) collective-permute-start(f32[9,4,128]{2,1,0:T(4,128)S(1)} %get-tuple-element.40), channel_id=1, source_target_pairs={{0,96},{32,64},{64,32},{96,0},{1,97},{33,65},{65,33},{97,1},{2,98}... | collective-permute-start | bytes 55304 | tf_op jit(solution)/shard_map/ppermute | solution.py:636
  28.9 13.7 %collective-permute-start.3 = (f32[9,4,128]{2,1,0:T(4,128)S(1)}, f32[9,4,128]{2,1,0:T(4,128)S(1)}, u32[]{:S(2)}, u32[]{:S(2)}) collective-permute-start(f32[9,4,128]{2,1,0:T(4,128)S(1)} %get-tuple-element.41), channel_id=1, source_target_pairs={{0,32},{32,0},{64,96},{96,64},{1,33},{33,1},{65,97},{97,65},{2,34}... | collective-permute-start | bytes 55304 | tf_op jit(solution)/shard_map/ppermute | solution.py:636
  31.1 5.5 %collective-permute-start.1 = (f32[8,128]{1,0:T(8,128)S(1)}, f32[8,128]{1,0:T(8,128)S(1)}, u32[]{:S(2)}, u32[]{:S(2)}) collective-permute-start(f32[8,128]{1,0:T(8,128)S(1)} %get-tuple-element.39), channel_id=1, source_target_pairs={{0,31},{1,2},{2,1},{3,4},{4,3},{5,6},{6,5},{7,8},{8,7},{9,10},{10,... | collective-permute-start | bytes 12296 | tf_op jit(solution)/shard_map/ppermute | solution.py:636
  36.6 6.0 %collective-permute-start.4 = (f32[8,128]{1,0:T(8,128)S(1)}, f32[8,128]{1,0:T(8,128)S(1)}, u32[]{:S(2)}, u32[]{:S(2)}) collective-permute-start(f32[8,128]{1,0:T(8,128)S(1)} %get-tuple-element.42), channel_id=1, source_target_pairs={{0,1},{1,0},{2,3},{3,2},{4,5},{5,4},{6,7},{7,6},{8,9},{9,8},{10,11... | collective-permute-start | bytes 12296 | tf_op jit(solution)/shard_map/ppermute | solution.py:636
  43.2 20.0 %collective-permute-start.6 = (f32[13,8,128]{2,1,0:T(8,128)S(1)}, f32[13,8,128]{2,1,0:T(8,128)S(1)}, u32[]{:S(2)}, u32[]{:S(2)}) collective-permute-start(f32[13,8,128]{2,1,0:T(8,128)S(1)} %get-tuple-element.48), channel_id=1, source_target_pairs={{0,896},{128,256},{256,128},{384,512},{512,384},{640,768},{768,640... | collective-permute-start | bytes 159752 | tf_op jit(solution)/shard_map/ppermute | solution.py:636
  49.2 13.9 %collective-permute-start.9 = (f32[13,8,128]{2,1,0:T(8,128)S(1)}, f32[13,8,128]{2,1,0:T(8,128)S(1)}, u32[]{:S(2)}, u32[]{:S(2)}) collective-permute-start(f32[13,8,128]{2,1,0:T(8,128)S(1)} %get-tuple-element.51), channel_id=1, source_target_pairs={{0,128},{128,0},{256,384},{384,256},{512,640},{640,512},{768,896},... | collective-permute-start | bytes 159752 | tf_op jit(solution)/shard_map/ppermute | solution.py:636
  54.4 7.0 %collective-permute-start.7 = (f32[13,4,128]{2,1,0:T(4,128)S(1)}, f32[13,4,128]{2,1,0:T(4,128)S(1)}, u32[]{:S(2)}, u32[]{:S(2)}) collective-permute-start(f32[13,4,128]{2,1,0:T(4,128)S(1)} %get-tuple-element.49), channel_id=1, source_target_pairs={{0,96},{32,64},{64,32},{96,0},{1,97},{33,65},{65,33},{97,1},{2,98}... | collective-permute-start | bytes 79880 | tf_op jit(solution)/shard_map/ppermute | solution.py:636
  57.4 5.7 %collective-permute-start.8 = (f32[13,4,128]{2,1,0:T(4,128)S(1)}, f32[13,4,128]{2,1,0:T(4,128)S(1)}, u32[]{:S(2)}, u32[]{:S(2)}) collective-permute-start(f32[13,4,128]{2,1,0:T(4,128)S(1)} %get-tuple-element.50), channel_id=1, source_target_pairs={{0,32},{32,0},{64,96},{96,64},{1,33},{33,1},{65,97},{97,65},{2,34}... | collective-permute-start | bytes 79880 | tf_op jit(solution)/shard_map/ppermute | solution.py:636
  63.4 17.4 %collective-permute-start.12 = (f32[10,128]{1,0:T(8,128)S(1)}, f32[10,128]{1,0:T(8,128)S(1)}, u32[]{:S(2)}, u32[]{:S(2)}) collective-permute-start(f32[10,128]{1,0:T(8,128)S(1)} %get-tuple-element.57), channel_id=1, source_target_pairs={{0,96},{32,64},{64,32},{96,0},{1,97},{33,65},{65,33},{97,1},{2,98}... | collective-permute-start | bytes 15368 | tf_op jit(solution)/shard_map/ppermute | solution.py:636
  67.5 13.4 %collective-permute-start.13 = (f32[10,128]{1,0:T(8,128)S(1)}, f32[10,128]{1,0:T(8,128)S(1)}, u32[]{:S(2)}, u32[]{:S(2)}) collective-permute-start(f32[10,128]{1,0:T(8,128)S(1)} %get-tuple-element.58), channel_id=1, source_target_pairs={{0,32},{32,0},{64,96},{96,64},{1,33},{33,1},{65,97},{97,65},{2,34}... | collective-permute-start | bytes 15368 | tf_op jit(solution)/shard_map/ppermute | solution.py:636
  70.0 9.3 %collective-permute-start.10 = (f32[8,128]{1,0:T(8,128)S(1)}, f32[8,128]{1,0:T(8,128)S(1)}, u32[]{:S(2)}, u32[]{:S(2)}) collective-permute-start(f32[8,128]{1,0:T(8,128)S(1)} %get-tuple-element.55), channel_id=1, source_target_pairs={{0,31},{1,2},{2,1},{3,4},{4,3},{5,6},{6,5},{7,8},{8,7},{9,10},{10,... | collective-permute-start | bytes 12296 | tf_op jit(solution)/shard_map/ppermute | solution.py:636
  74.3 6.5 %collective-permute-start.11 = (f32[8,128]{1,0:T(8,128)S(1)}, f32[8,128]{1,0:T(8,128)S(1)}, u32[]{:S(2)}, u32[]{:S(2)}) collective-permute-start(f32[8,128]{1,0:T(8,128)S(1)} %get-tuple-element.56), channel_id=1, source_target_pairs={{0,1},{1,0},{2,3},{3,2},{4,5},{5,4},{6,7},{7,6},{8,9},{9,8},{10,11... | collective-permute-start | bytes 12296 | tf_op jit(solution)/shard_map/ppermute | solution.py:636
  100.6 14.6 %collective-permute-start.14 = (f32[1,128]{1,0:T(1,128)S(1)}, f32[1,128]{1,0:T(1,128)S(1)}, u32[]{:S(2)}, u32[]{:S(2)}) collective-permute-start(f32[1,128]{1,0:T(1,128)S(1)} %bitcast_select_fusion.3), channel_id=1, source_target_pairs={{0,788},{1,793},{2,798},{3,3},{4,792},{5,797},{6,2},{7,7},{8,796},... | collective-permute-start | bytes 1544 | tf_op jit(solution)/shard_map/ppermute | solution.py:660
where the time goes:
time: 149 us; the launch traced here: 148 us
  starting transfers between devices  83.2 us (56%)
  blocking collectives  51.3 us (34%)
  waiting for transfers between devices  8.5 us (6%)
  Pallas kernels  3.8 us (3%)
    ppermute x14, starting transfers between devices, exchange(): lax.ppermute(message, axis, [(a, partner(a, size)) for a in range(size)])  69.9 us
    all_gather x6, blocking collectives, gather(): every = lax.all_gather(stat, axis, tiled=True)  51.3 us
    ppermute x1, starting transfers between devices, spread(): return lax.ppermute(stat, names, pairs)  13.3 us
    ppermute x14, waiting for transfers between devices, exchange(): lax.ppermute(message, axis, [(a, partner(a, size)) for a in range(size)])  7.86 us
    pallas_call x6, Pallas kernels, run(): pl.pallas_call(kernel, in_specs=[pl.BlockSpec(memory_space=pltpu.VMEM)] *...  3.8 us
  transfers between devices with their start and end apart: 15, of which 6 were waited for; matrix products, arithmetic and copies ran while one was open for 0% of the time, Pallas kernels for 0%

commit v1 on v0

--- a/solution.py
+++ b/solution.py
@@ -431,7 +431,7 @@
     return [field[first + c][x] for c in range(count)]
 
 
-def join_kernel(f1_ref, f2_ref, xo, yo, yp, xp, f2_out, side_ref, row_ref, zo, zp, eo, ep):
+def join_kernel(f1_ref, f2_ref, xo, yo, yp, xp, f2_out, side_ref, row_ref, zo, eo, ep, zp):
     even = is_even()
     y = Line(0)
     f1, f2 = (load(f1_ref), load(f2_ref))
@@ -489,7 +489,7 @@
 
 
 def last_kernel(
-    u_ref, rate_ref, fast_ref, f1_ref, f2_ref, side_ref, row_ref, zo, zp, eo, ep, next_ref, stat_ref
+    u_ref, rate_ref, fast_ref, f1_ref, f2_ref, side_ref, row_ref, zo, eo, ep, zp, next_ref, stat_ref
 ):
     even = is_even()
     y, z = (Line(0), Line(1))
@@ -625,7 +625,7 @@
         (GX, pair_of),
     ),
     "second": ((GX, other_of), ("gy", other_of), ("gy", pair_of), (GX, pair_of)),
-    "third": ((GZ, other_of), (GZ, pair_of), ("gy", other_of), ("gy", pair_of)),
+    "third": ((GZ, other_of), ("gy", other_of), ("gy", pair_of), (GZ, pair_of)),
 }
 
 
@@ -652,7 +652,11 @@
     pairs = []
     for at in np.ndindex(*sizes):
         a, core, b, c, e = at
-        place = (a * sizes[3] + c + core * sizes[4] + e - (sizes[3] // 2 - 1)) % ring
+        half = sizes[4] // 2
+        step = e - (half - 1)
+        if core:
+            step += half if step > 0 else -half
+        place = (a * sizes[3] + c + step) % ring
         to = (place // sizes[3], core, b, place % sizes[3], e)
         pairs.append(
             (int(np.ravel_multi_index(at, sizes)), int(np.ravel_multi_index(to, sizes)))
@@ -701,7 +705,7 @@
     corners = shape(10, NZ)
     f2, sides, rows, *messages = call(
         join_kernel,
-        [shape(8, *full), shape(2, 13, NY, NZ), shape(13, *full), tile, tile, corners, corners],
+        [shape(8, *full), shape(2, 13, NY, NZ), shape(13, *full), tile, corners, corners, tile],
         10**6,
     )(f1, f2, *received)
     received = exchange(messages, "third")

time: 149 us -> 150 us (level)
  the two profiles are of different devices: /device:TPU:72 before, /device:TPU:8 now
where the time goes in v1:
time: 150 us; the launch traced here: 149 us
  starting transfers between devices  81.7 us (54%)
  blocking collectives  54.3 us (36%)
  waiting for transfers between devices  7.87 us (5%)
  Pallas kernels  3.8 us (3%)
    ppermute x14, starting transfers between devices, exchange(): lax.ppermute(message, axis, [(a, partner(a, size)) for a in range(size)])  81 us
    all_gather x6, blocking collectives, gather(): every = lax.all_gather(stat, axis, tiled=True)  54.3 us
    ppermute x14, waiting for transfers between devices, exchange(): lax.ppermute(message, axis, [(a, partner(a, size)) for a in range(size)])  7.86 us
    pallas_call x6, Pallas kernels, run(): pl.pallas_call(kernel, in_specs=[pl.BlockSpec(memory_space=pltpu.VMEM)] *...  3.8 us
  transfers between devices with their start and end apart: 15, of which 5 were waited for; matrix products, arithmetic and copies ran while one was open for 0% of the time, Pallas kernels for 0%

profile of v1, /device:TPU:8, one launch (start us, length us, event | category | flops | bytes accessed | tf_op | source)
XLA Modules:
  0.0 149.3 jit_solution(180177322214218776)
XLA Ops:
  0.6 1.0 shard_map.57
  1.7 22.4 %collective-permute-start = (f32[9,8,128]{2,1,0:T(8,128)S(1)}, f32[9,8,128]{2,1,0:T(8,128)S(1)}, u32[]{:S(2)}, u32[]{:S(2)}) collective-permute-start(f32[9,8,128]{2,1,0:T(8,128)S(1)} %get-tuple-element.38), channel_id=1, source_target_pairs={{0,896},{128,256},{256,128},{384,512},{512,384},{640,768},{768,640... | collective-permute-start | bytes 110600 | tf_op jit(solution)/shard_map/ppermute | solution.py:636
  24.1 1.9 %collective-permute-start.5 = (f32[9,8,128]{2,1,0:T(8,128)S(1)}, f32[9,8,128]{2,1,0:T(8,128)S(1)}, u32[]{:S(2)}, u32[]{:S(2)}) collective-permute-start(f32[9,8,128]{2,1,0:T(8,128)S(1)} %get-tuple-element.43), channel_id=1, source_target_pairs={{0,128},{128,0},{256,384},{384,256},{512,640},{640,512},{768,896},... | collective-permute-start | bytes 110600 | tf_op jit(solution)/shard_map/ppermute | solution.py:636
  26.0 4.7 %collective-permute-start.2 = (f32[9,4,128]{2,1,0:T(4,128)S(1)}, f32[9,4,128]{2,1,0:T(4,128)S(1)}, u32[]{:S(2)}, u32[]{:S(2)}) collective-permute-start(f32[9,4,128]{2,1,0:T(4,128)S(1)} %get-tuple-element.40), channel_id=1, source_target_pairs={{0,96},{32,64},{64,32},{96,0},{1,97},{33,65},{65,33},{97,1},{2,98}... | collective-permute-start | bytes 55304 | tf_op jit(solution)/shard_map/ppermute | solution.py:636
  30.7 2.1 %collective-permute-start.3 = (f32[9,4,128]{2,1,0:T(4,128)S(1)}, f32[9,4,128]{2,1,0:T(4,128)S(1)}, u32[]{:S(2)}, u32[]{:S(2)}) collective-permute-start(f32[9,4,128]{2,1,0:T(4,128)S(1)} %get-tuple-element.41), channel_id=1, source_target_pairs={{0,32},{32,0},{64,96},{96,64},{1,33},{33,1},{65,97},{97,65},{2,34}... | collective-permute-start | bytes 55304 | tf_op jit(solution)/shard_map/ppermute | solution.py:636
  32.9 3.5 %collective-permute-start.1 = (f32[8,128]{1,0:T(8,128)S(1)}, f32[8,128]{1,0:T(8,128)S(1)}, u32[]{:S(2)}, u32[]{:S(2)}) collective-permute-start(f32[8,128]{1,0:T(8,128)S(1)} %get-tuple-element.39), channel_id=1, source_target_pairs={{0,31},{1,2},{2,1},{3,4},{4,3},{5,6},{6,5},{7,8},{8,7},{9,10},{10,... | collective-permute-start | bytes 12296 | tf_op jit(solution)/shard_map/ppermute | solution.py:636
  36.4 2.0 %collective-permute-done.1.refs_1_ = f32[8,128]{1,0:T(8,128)S(1)} collective-permute-done((f32[8,128]{1,0:T(8,128)S(1)}, f32[8,128]{1,0:T(8,128)S(1)}, u32[]{:S(2)}, u32[]{:S(2)}) %collective-permute-start.1) | collective-permute-done | bytes 4128 | tf_op jit(solution)/shard_map/ppermute | solution.py:636
  38.4 11.1 %collective-permute-start.4 = (f32[8,128]{1,0:T(8,128)S(1)}, f32[8,128]{1,0:T(8,128)S(1)}, u32[]{:S(2)}, u32[]{:S(2)}) collective-permute-start(f32[8,128]{1,0:T(8,128)S(1)} %get-tuple-element.42), channel_id=1, source_target_pairs={{0,1},{1,0},{2,3},{3,2},{4,5},{5,4},{6,7},{7,6},{8,9},{9,8},{10,11... | collective-permute-start | bytes 12296 | tf_op jit(solution)/shard_map/ppermute | solution.py:636
  49.4 0.4 shard_map.58
  49.9 1.1 collective-permute-done.4.refs_4_
  51.0 0.0 collective-permute-done.2.refs_2_
  51.0 0.0 collective-permute-done.3.refs_3_
  51.0 0.0 collective-permute-done.refs_0_
  51.0 0.0 collective-permute-done.5.refs_5_
  51.0 0.6 shard_map.59
  51.6 6.0 %collective-permute-start.6 = (f32[13,8,128]{2,1,0:T(8,128)S(1)}, f32[13,8,128]{2,1,0:T(8,128)S(1)}, u32[]{:S(2)}, u32[]{:S(2)}) collective-permute-start(f32[13,8,128]{2,1,0:T(8,128)S(1)} %get-tuple-element.48), channel_id=1, source_target_pairs={{0,896},{128,256},{256,128},{384,512},{512,384},{640,768},{768,640... | collective-permute-start | bytes 159752 | tf_op jit(solution)/shard_map/ppermute | solution.py:636
  57.6 5.1 %collective-permute-start.9 = (f32[13,8,128]{2,1,0:T(8,128)S(1)}, f32[13,8,128]{2,1,0:T(8,128)S(1)}, u32[]{:S(2)}, u32[]{:S(2)}) collective-permute-start(f32[13,8,128]{2,1,0:T(8,128)S(1)} %get-tuple-element.51), channel_id=1, source_target_pairs={{0,128},{128,0},{256,384},{384,256},{512,640},{640,512},{768,896},... | collective-permute-start | bytes 159752 | tf_op jit(solution)/shard_map/ppermute | solution.py:636
  62.8 3.0 %collective-permute-start.7 = (f32[13,4,128]{2,1,0:T(4,128)S(1)}, f32[13,4,128]{2,1,0:T(4,128)S(1)}, u32[]{:S(2)}, u32[]{:S(2)}) collective-permute-start(f32[13,4,128]{2,1,0:T(4,128)S(1)} %get-tuple-element.49), channel_id=1, source_target_pairs={{0,96},{32,64},{64,32},{96,0},{1,97},{33,65},{65,33},{97,1},{2,98}... | collective-permute-start | bytes 79880 | tf_op jit(solution)/shard_map/ppermute | solution.py:636
  65.8 2.6 %collective-permute-start.8 = (f32[13,4,128]{2,1,0:T(4,128)S(1)}, f32[13,4,128]{2,1,0:T(4,128)S(1)}, u32[]{:S(2)}, u32[]{:S(2)}) collective-permute-start(f32[13,4,128]{2,1,0:T(4,128)S(1)} %get-tuple-element.50), channel_id=1, source_target_pairs={{0,32},{32,0},{64,96},{96,64},{1,33},{33,1},{65,97},{97,65},{2,34}... | collective-permute-start | bytes 79880 | tf_op jit(solution)/shard_map/ppermute | solution.py:636
  68.4 1.3 collective-permute-done.7.yo
  69.7 1.8 %collective-permute-done.8.yp = f32[13,4,128]{2,1,0:T(4,128)S(1)} collective-permute-done((f32[13,4,128]{2,1,0:T(4,128)S(1)}, f32[13,4,128]{2,1,0:T(4,128)S(1)}, u32[]{:S(2)}, u32[]{:S(2)}) %collective-permute-start.8) | collective-permute-done | bytes 26656 | tf_op jit(solution)/shard_map/ppermute | solution.py:636
  71.6 0.0 collective-permute-done.6.xo
  71.6 0.0 collective-permute-done.9.xp
  71.6 0.3 shard_map.60
  71.8 4.0 %collective-permute-start.11 = (f32[10,128]{1,0:T(8,128)S(1)}, f32[10,128]{1,0:T(8,128)S(1)}, u32[]{:S(2)}, u32[]{:S(2)}) collective-permute-start(f32[10,128]{1,0:T(8,128)S(1)} %get-tuple-element.56), channel_id=1, source_target_pairs={{0,96},{32,64},{64,32},{96,0},{1,97},{33,65},{65,33},{97,1},{2,98}... | collective-permute-start | bytes 15368 | tf_op jit(solution)/shard_map/ppermute | solution.py:636
  75.9 2.5 %collective-permute-start.12 = (f32[10,128]{1,0:T(8,128)S(1)}, f32[10,128]{1,0:T(8,128)S(1)}, u32[]{:S(2)}, u32[]{:S(2)}) collective-permute-start(f32[10,128]{1,0:T(8,128)S(1)} %get-tuple-element.57), channel_id=1, source_target_pairs={{0,32},{32,0},{64,96},{96,64},{1,33},{33,1},{65,97},{97,65},{2,34}... | collective-permute-start | bytes 15368 | tf_op jit(solution)/shard_map/ppermute | solution.py:636
  78.4 1.9 %collective-permute-start.10 = (f32[8,128]{1,0:T(8,128)S(1)}, f32[8,128]{1,0:T(8,128)S(1)}, u32[]{:S(2)}, u32[]{:S(2)}) collective-permute-start(f32[8,128]{1,0:T(8,128)S(1)} %get-tuple-element.55), channel_id=1, source_target_pairs={{0,31},{1,2},{2,1},{3,4},{4,3},{5,6},{6,5},{7,8},{8,7},{9,10},{10,... | collective-permute-start | bytes 12296 | tf_op jit(solution)/shard_map/ppermute | solution.py:636
  80.3 10.1 %collective-permute-start.13 = (f32[8,128]{1,0:T(8,128)S(1)}, f32[8,128]{1,0:T(8,128)S(1)}, u32[]{:S(2)}, u32[]{:S(2)}) collective-permute-start(f32[8,128]{1,0:T(8,128)S(1)} %get-tuple-element.58), channel_id=1, source_target_pairs={{0,1},{1,0},{2,3},{3,2},{4,5},{5,4},{6,7},{7,6},{8,9},{9,8},{10,11... | collective-permute-start | bytes 12296 | tf_op jit(solution)/shard_map/ppermute | solution.py:636
  90.4 0.0 collective-permute-done.10.zo
  90.4 1.6 %collective-permute-done.13.zp = f32[8,128]{1,0:T(8,128)S(1)} collective-permute-done((f32[8,128]{1,0:T(8,128)S(1)}, f32[8,128]{1,0:T(8,128)S(1)}, u32[]{:S(2)}, u32[]{:S(2)}) %collective-permute-start.13) | collective-permute-done | bytes 4128 | tf_op jit(solution)/shard_map/ppermute | solution.py:636
  92.0 0.0 collective-permute-done.11.eo
  92.0 0.0 collective-permute-done.12.ep
  92.0 0.5 shard_map.61
  92.5 1.8 %all-gather = f32[2,1,128]{2,1,0:T(1,128)S(1)} all-gather(f32[1,1,128]{2,1,0:T(1,128)S(1)} %bitcast.43), channel_id=1, replica_groups=mesh['gx_0'=4,'gx_1'=2,'gy'=4,'gz_0'=8,'gz_1'=4] {'gx_1'}, dimensions={0}, use_global_device_ids=true | all-gather | bytes 1536 | tf_op jit(solution)/shard_map/all_gather | solution.py:642
  94.3 8.4 %all-gather.1 = f32[4,1,128]{2,1,0:T(1,128)S(1)} all-gather(f32[1,1,128]{2,1,0:T(1,128)S(1)} %fusion.3), channel_id=1, replica_groups=mesh['gx_0'=4,'gx_1'=2,'gy'=4,'gz_0'=8,'gz_1'=4] {'gy'}, dimensions={0}, use_global_device_ids=true | all-gather | bytes 2560 | tf_op jit(solution)/shard_map/all_gather | solution.py:642
  102.8 9.6 %all-gather.2 = f32[4,1,128]{2,1,0:T(1,128)S(1)} all-gather(f32[1,1,128]{2,1,0:T(1,128)S(1)} %fusion.2), channel_id=1, replica_groups=mesh['gx_0'=4,'gx_1'=2,'gy'=4,'gz_0'=8,'gz_1'=4] {'gz_1'}, dimensions={0}, use_global_device_ids=true | all-gather | bytes 2560 | tf_op jit(solution)/shard_map/all_gather | solution.py:642
  112.4 0.7 collective-permute-start.14
  113.1 0.6 copy.6
  113.7 0.0 collective-permute-done.14
  113.7 1.8 %all-gather.3 = f32[2,1,128]{2,1,0:T(1,128)S(1)} all-gather(f32[1,1,128]{2,1,0:T(1,128)S(1)} %bitcast.44), channel_id=1, replica_groups=mesh['gx_0'=4,'gx_1'=2,'gy'=4,'gz_0'=8,'gz_1'=4] {'gx_1'}, dimensions={0}, use_global_device_ids=true | all-gather | bytes 1536 | tf_op jit(solution)/shard_map/all_gather | solution.py:642
  115.5 12.0 %all-gather.4 = f32[4,1,128]{2,1,0:T(1,128)S(1)} all-gather(f32[1,1,128]{2,1,0:T(1,128)S(1)} %fusion.1), channel_id=1, replica_groups=mesh['gx_0'=4,'gx_1'=2,'gy'=4,'gz_0'=8,'gz_1'=4] {'gz_1'}, dimensions={0}, use_global_device_ids=true | all-gather | bytes 2560 | tf_op jit(solution)/shard_map/all_gather | solution.py:642
  127.6 20.7 %all-gather.5 = f32[4,1,128]{2,1,0:T(1,128)S(1)} all-gather(f32[1,1,128]{2,1,0:T(1,128)S(1)} %fusion), channel_id=1, replica_groups=mesh['gx_0'=4,'gx_1'=2,'gy'=4,'gz_0'=8,'gz_1'=4] {'gx_0'}, dimensions={0}, use_global_device_ids=true | all-gather | bytes 2560 | tf_op jit(solution)/shard_map/all_gather | solution.py:642
  148.3 0.9 shard_map.62
  (12 shorter events, 0.2 us)
Async XLA Ops:
  1.7 49.3 %collective-permute-start = (f32[9,8,128]{2,1,0:T(8,128)S(1)}, f32[9,8,128]{2,1,0:T(8,128)S(1)}, u32[]{:S(2)}, u32[]{:S(2)}) collective-permute-start(f32[9,8,128]{2,1,0:T(8,128)S(1)} %get-tuple-element.38), channel_id=1, source_target_pairs={{0,896},{128,256},{256,128},{384,512},{512,384},{640,768},{768,640... | collective-permute-start | bytes 110600 | tf_op jit(solution)/shard_map/ppermute | solution.py:636
  24.1 26.9 %collective-permute-start.5 = (f32[9,8,128]{2,1,0:T(8,128)S(1)}, f32[9,8,128]{2,1,0:T(8,128)S(1)}, u32[]{:S(2)}, u32[]{:S(2)}) collective-permute-start(f32[9,8,128]{2,1,0:T(8,128)S(1)} %get-tuple-element.43), channel_id=1, source_target_pairs={{0,128},{128,0},{256,384},{384,256},{512,640},{640,512},{768,896},... | collective-permute-start | bytes 110600 | tf_op jit(solution)/shard_map/ppermute | solution.py:636
  26.0 25.0 %collective-permute-start.2 = (f32[9,4,128]{2,1,0:T(4,128)S(1)}, f32[9,4,128]{2,1,0:T(4,128)S(1)}, u32[]{:S(2)}, u32[]{:S(2)}) collective-permute-start(f32[9,4,128]{2,1,0:T(4,128)S(1)} %get-tuple-element.40), channel_id=1, source_target_pairs={{0,96},{32,64},{64,32},{96,0},{1,97},{33,65},{65,33},{97,1},{2,98}... | collective-permute-start | bytes 55304 | tf_op jit(solution)/shard_map/ppermute | solution.py:636
  30.7 20.3 %collective-permute-start.3 = (f32[9,4,128]{2,1,0:T(4,128)S(1)}, f32[9,4,128]{2,1,0:T(4,128)S(1)}, u32[]{:S(2)}, u32[]{:S(2)}) collective-permute-start(f32[9,4,128]{2,1,0:T(4,128)S(1)} %get-tuple-element.41), channel_id=1, source_target_pairs={{0,32},{32,0},{64,96},{96,64},{1,33},{33,1},{65,97},{97,65},{2,34}... | collective-permute-start | bytes 55304 | tf_op jit(solution)/shard_map/ppermute | solution.py:636
  32.9 5.5 %collective-permute-start.1 = (f32[8,128]{1,0:T(8,128)S(1)}, f32[8,128]{1,0:T(8,128)S(1)}, u32[]{:S(2)}, u32[]{:S(2)}) collective-permute-start(f32[8,128]{1,0:T(8,128)S(1)} %get-tuple-element.39), channel_id=1, source_target_pairs={{0,31},{1,2},{2,1},{3,4},{4,3},{5,6},{6,5},{7,8},{8,7},{9,10},{10,... | collective-permute-start | bytes 12296 | tf_op jit(solution)/shard_map/ppermute | solution.py:636
  38.4 12.6 %collective-permute-start.4 = (f32[8,128]{1,0:T(8,128)S(1)}, f32[8,128]{1,0:T(8,128)S(1)}, u32[]{:S(2)}, u32[]{:S(2)}) collective-permute-start(f32[8,128]{1,0:T(8,128)S(1)} %get-tuple-element.42), channel_id=1, source_target_pairs={{0,1},{1,0},{2,3},{3,2},{4,5},{5,4},{6,7},{7,6},{8,9},{9,8},{10,11... | collective-permute-start | bytes 12296 | tf_op jit(solution)/shard_map/ppermute | solution.py:636
  51.6 20.0 %collective-permute-start.6 = (f32[13,8,128]{2,1,0:T(8,128)S(1)}, f32[13,8,128]{2,1,0:T(8,128)S(1)}, u32[]{:S(2)}, u32[]{:S(2)}) collective-permute-start(f32[13,8,128]{2,1,0:T(8,128)S(1)} %get-tuple-element.48), channel_id=1, source_target_pairs={{0,896},{128,256},{256,128},{384,512},{512,384},{640,768},{768,640... | collective-permute-start | bytes 159752 | tf_op jit(solution)/shard_map/ppermute | solution.py:636
  57.6 13.9 %collective-permute-start.9 = (f32[13,8,128]{2,1,0:T(8,128)S(1)}, f32[13,8,128]{2,1,0:T(8,128)S(1)}, u32[]{:S(2)}, u32[]{:S(2)}) collective-permute-start(f32[13,8,128]{2,1,0:T(8,128)S(1)} %get-tuple-element.51), channel_id=1, source_target_pairs={{0,128},{128,0},{256,384},{384,256},{512,640},{640,512},{768,896},... | collective-permute-start | bytes 159752 | tf_op jit(solution)/shard_map/ppermute | solution.py:636
  62.8 7.0 %collective-permute-start.7 = (f32[13,4,128]{2,1,0:T(4,128)S(1)}, f32[13,4,128]{2,1,0:T(4,128)S(1)}, u32[]{:S(2)}, u32[]{:S(2)}) collective-permute-start(f32[13,4,128]{2,1,0:T(4,128)S(1)} %get-tuple-element.49), channel_id=1, source_target_pairs={{0,96},{32,64},{64,32},{96,0},{1,97},{33,65},{65,33},{97,1},{2,98}... | collective-permute-start | bytes 79880 | tf_op jit(solution)/shard_map/ppermute | solution.py:636
  65.8 5.7 %collective-permute-start.8 = (f32[13,4,128]{2,1,0:T(4,128)S(1)}, f32[13,4,128]{2,1,0:T(4,128)S(1)}, u32[]{:S(2)}, u32[]{:S(2)}) collective-permute-start(f32[13,4,128]{2,1,0:T(4,128)S(1)} %get-tuple-element.50), channel_id=1, source_target_pairs={{0,32},{32,0},{64,96},{96,64},{1,33},{33,1},{65,97},{97,65},{2,34}... | collective-permute-start | bytes 79880 | tf_op jit(solution)/shard_map/ppermute | solution.py:636
  71.8 20.1 %collective-permute-start.11 = (f32[10,128]{1,0:T(8,128)S(1)}, f32[10,128]{1,0:T(8,128)S(1)}, u32[]{:S(2)}, u32[]{:S(2)}) collective-permute-start(f32[10,128]{1,0:T(8,128)S(1)} %get-tuple-element.56), channel_id=1, source_target_pairs={{0,96},{32,64},{64,32},{96,0},{1,97},{33,65},{65,33},{97,1},{2,98}... | collective-permute-start | bytes 15368 | tf_op jit(solution)/shard_map/ppermute | solution.py:636
  75.9 16.1 %collective-permute-start.12 = (f32[10,128]{1,0:T(8,128)S(1)}, f32[10,128]{1,0:T(8,128)S(1)}, u32[]{:S(2)}, u32[]{:S(2)}) collective-permute-start(f32[10,128]{1,0:T(8,128)S(1)} %get-tuple-element.57), channel_id=1, source_target_pairs={{0,32},{32,0},{64,96},{96,64},{1,33},{33,1},{65,97},{97,65},{2,34}... | collective-permute-start | bytes 15368 | tf_op jit(solution)/shard_map/ppermute | solution.py:636
  78.4 12.0 %collective-permute-start.10 = (f32[8,128]{1,0:T(8,128)S(1)}, f32[8,128]{1,0:T(8,128)S(1)}, u32[]{:S(2)}, u32[]{:S(2)}) collective-permute-start(f32[8,128]{1,0:T(8,128)S(1)} %get-tuple-element.55), channel_id=1, source_target_pairs={{0,31},{1,2},{2,1},{3,4},{4,3},{5,6},{6,5},{7,8},{8,7},{9,10},{10,... | collective-permute-start | bytes 12296 | tf_op jit(solution)/shard_map/ppermute | solution.py:636
  80.3 11.7 %collective-permute-start.13 = (f32[8,128]{1,0:T(8,128)S(1)}, f32[8,128]{1,0:T(8,128)S(1)}, u32[]{:S(2)}, u32[]{:S(2)}) collective-permute-start(f32[8,128]{1,0:T(8,128)S(1)} %get-tuple-element.58), channel_id=1, source_target_pairs={{0,1},{1,0},{2,3},{3,2},{4,5},{5,4},{6,7},{7,6},{8,9},{9,8},{10,11... | collective-permute-start | bytes 12296 | tf_op jit(solution)/shard_map/ppermute | solution.py:636
  112.4 1.3 collective-permute-start.14

commit v2 on v0

--- a/solution.py
+++ b/solution.py
@@ -431,7 +431,7 @@
     return [field[first + c][x] for c in range(count)]
 
 
-def join_kernel(f1_ref, f2_ref, xo, yo, yp, xp, f2_out, side_ref, row_ref, zo, zp, eo, ep):
+def join_kernel(f1_ref, f2_ref, xo, yo, yp, xp, f2_out, side_ref, row_ref, zo, zp, corner_ref):
     even = is_even()
     y = Line(0)
     f1, f2 = (load(f1_ref), load(f2_ref))
@@ -466,9 +466,8 @@
         for c in range(13):
             side_ref[w, c] = side[c]
         for c in range(5):
-            low, high = (side[c][0:1, :], side[c][NY - 1 : NY, :])
-            eo[pl.ds(5 * w + c, 1), :] = jnp.where(even[1], low, high)
-            ep[pl.ds(5 * w + c, 1), :] = jnp.where(even[1], high, low)
+            corner_ref[0, pl.ds(5 * w + c, 1), :] = side[c][0:1, :]
+            corner_ref[1, pl.ds(5 * w + c, 1), :] = side[c][NY - 1 : NY, :]
     pack_z(flat(f1 + f2) + sides[0][:5] + sides[1][:5] + flat(rows[:5]), zo, zp)
 
 
@@ -489,12 +488,15 @@
 
 
 def last_kernel(
-    u_ref, rate_ref, fast_ref, f1_ref, f2_ref, side_ref, row_ref, zo, zp, eo, ep, next_ref, stat_ref
+    u_ref, rate_ref, fast_ref, f1_ref, f2_ref, side_ref, row_ref, zo, zp, corner_ref, next_ref, stat_ref
 ):
     even = is_even()
     y, z = (Line(0), Line(1))
     f1, f2, rows = (load(f1_ref), load(f2_ref), load(row_ref))
     sides = [[side_ref[w, c] for c in range(13)] for w in range(2)]
+    places = lax.axis_size("gy")
+    below = lax.rem(lax.axis_index("gy") + (places - 1), places)
+    above = lax.rem(lax.axis_index("gy") + 1, places)
     z_other, z_pair = (zo[...], zp[...])
     z_low = jnp.where(even[2], z_other, z_pair)
     z_high = jnp.where(even[2], z_pair, z_other)
@@ -518,10 +520,13 @@
     for w, x, sign in ((0, 0, -6.0), (1, NX - 1, 6.0)):
         corner = []
         for c in range(5):
-            other, pair = (eo[pl.ds(5 * w + c, 1), :], ep[pl.ds(5 * w + c, 1), :])
-            low = jnp.broadcast_to(jnp.where(even[1], other, pair), (NY, NZ))
-            high = jnp.broadcast_to(jnp.where(even[1], pair, other), (NY, NZ))
-            corner.append(jnp.where(y.lowest, low, high))
+            low = corner_ref[2 * below + 1, pl.ds(5 * w + c, 1), :]
+            high = corner_ref[2 * above, pl.ds(5 * w + c, 1), :]
+            corner.append(
+                jnp.where(
+                    y.lowest, jnp.broadcast_to(low, (NY, NZ)), jnp.broadcast_to(high, (NY, NZ))
+                )
+            )
         side = sides[w]
         beside = [column(13 * NX + 5 * w + c) for c in range(5)]
         side[5:] = meet(side[5:], gaps(z_outer, beside, side[:5]), 2, z_sign)
@@ -625,7 +630,7 @@
         (GX, pair_of),
     ),
     "second": ((GX, other_of), ("gy", other_of), ("gy", pair_of), (GX, pair_of)),
-    "third": ((GZ, other_of), (GZ, pair_of), ("gy", other_of), ("gy", pair_of)),
+    "third": ((GZ, other_of), (GZ, pair_of)),
 }
 
 
@@ -698,15 +703,15 @@
         10**6,
     )(u, g, vol, alpha, *received)
     received = exchange(messages, "second")
-    corners = shape(10, NZ)
-    f2, sides, rows, *messages = call(
+    f2, sides, rows, *messages, corners = call(
         join_kernel,
-        [shape(8, *full), shape(2, 13, NY, NZ), shape(13, *full), tile, tile, corners, corners],
+        [shape(8, *full), shape(2, 13, NY, NZ), shape(13, *full), tile, tile, shape(2, 10, NZ)],
         10**6,
     )(f1, f2, *received)
     received = exchange(messages, "third")
+    corners = lax.all_gather(corners, "gy", tiled=True)
     field, stat = call(last_kernel, [shape(8, *full), shape(1, NZ)], 10**6)(
-        u, rate, fast, f1, f2, sides, rows, *received
+        u, rate, fast, f1, f2, sides, rows, *received, corners
     )
     stat = over_all(stat)
     gravity, gravity_source, norm = call(

time: 149 us -> 153 us (1.027)
  the two profiles are of different devices: /device:TPU:72 before, /device:TPU:8 now
where the time goes in v2:
time: 153 us; the launch traced here: 152 us
  starting transfers between devices  76.4 us (50%)
  blocking collectives  60.3 us (39%)
  waiting for transfers between devices  10.1 us (7%)
  Pallas kernels  3.8 us (2%)
    ppermute x12, starting transfers between devices, exchange(): lax.ppermute(message, axis, [(a, partner(a, size)) for a in range(size)])  74.5 us
    all_gather x6, blocking collectives, gather(): every = lax.all_gather(stat, axis, tiled=True)  48.4 us
    all_gather x1, blocking collectives, local(): corners = lax.all_gather(corners, 'gy', tiled=True)  11.9 us
    ppermute x12, waiting for transfers between devices, exchange(): lax.ppermute(message, axis, [(a, partner(a, size)) for a in range(size)])  6.3 us
    pallas_call x6, Pallas kernels, run(): pl.pallas_call(kernel, in_specs=[pl.BlockSpec(memory_space=pltpu.VMEM)] *...  3.8 us
    ppermute x1, waiting for transfers between devices, spread(): return lax.ppermute(stat, names, pairs)  3.79 us
  transfers between devices with their start and end apart: 13, of which 5 were waited for; matrix products, arithmetic and copies ran while one was open for 0% of the time, Pallas kernels for 0%

profile of v2, /device:TPU:8, one launch (start us, length us, event | category | flops | bytes accessed | tf_op | source)
XLA Modules:
  0.0 152.2 jit_solution(11041774378217518534)
XLA Ops:
  0.6 1.0 shard_map.57
  1.7 22.4 %collective-permute-start = (f32[9,8,128]{2,1,0:T(8,128)S(1)}, f32[9,8,128]{2,1,0:T(8,128)S(1)}, u32[]{:S(2)}, u32[]{:S(2)}) collective-permute-start(f32[9,8,128]{2,1,0:T(8,128)S(1)} %get-tuple-element.37), channel_id=1, source_target_pairs={{0,896},{128,256},{256,128},{384,512},{512,384},{640,768},{768,640... | collective-permute-start | bytes 110600 | tf_op jit(solution)/shard_map/ppermute | solution.py:641
  24.1 1.9 %collective-permute-start.5 = (f32[9,8,128]{2,1,0:T(8,128)S(1)}, f32[9,8,128]{2,1,0:T(8,128)S(1)}, u32[]{:S(2)}, u32[]{:S(2)}) collective-permute-start(f32[9,8,128]{2,1,0:T(8,128)S(1)} %get-tuple-element.42), channel_id=1, source_target_pairs={{0,128},{128,0},{256,384},{384,256},{512,640},{640,512},{768,896},... | collective-permute-start | bytes 110600 | tf_op jit(solution)/shard_map/ppermute | solution.py:641
  26.0 4.7 %collective-permute-start.2 = (f32[9,4,128]{2,1,0:T(4,128)S(1)}, f32[9,4,128]{2,1,0:T(4,128)S(1)}, u32[]{:S(2)}, u32[]{:S(2)}) collective-permute-start(f32[9,4,128]{2,1,0:T(4,128)S(1)} %get-tuple-element.39), channel_id=1, source_target_pairs={{0,96},{32,64},{64,32},{96,0},{1,97},{33,65},{65,33},{97,1},{2,98}... | collective-permute-start | bytes 55304 | tf_op jit(solution)/shard_map/ppermute | solution.py:641
  30.7 2.1 %collective-permute-start.3 = (f32[9,4,128]{2,1,0:T(4,128)S(1)}, f32[9,4,128]{2,1,0:T(4,128)S(1)}, u32[]{:S(2)}, u32[]{:S(2)}) collective-permute-start(f32[9,4,128]{2,1,0:T(4,128)S(1)} %get-tuple-element.40), channel_id=1, source_target_pairs={{0,32},{32,0},{64,96},{96,64},{1,33},{33,1},{65,97},{97,65},{2,34}... | collective-permute-start | bytes 55304 | tf_op jit(solution)/shard_map/ppermute | solution.py:641
  32.9 3.5 %collective-permute-start.1 = (f32[8,128]{1,0:T(8,128)S(1)}, f32[8,128]{1,0:T(8,128)S(1)}, u32[]{:S(2)}, u32[]{:S(2)}) collective-permute-start(f32[8,128]{1,0:T(8,128)S(1)} %get-tuple-element.38), channel_id=1, source_target_pairs={{0,31},{1,2},{2,1},{3,4},{4,3},{5,6},{6,5},{7,8},{8,7},{9,10},{10,... | collective-permute-start | bytes 12296 | tf_op jit(solution)/shard_map/ppermute | solution.py:641
  36.4 2.0 %collective-permute-done.1.refs_1_ = f32[8,128]{1,0:T(8,128)S(1)} collective-permute-done((f32[8,128]{1,0:T(8,128)S(1)}, f32[8,128]{1,0:T(8,128)S(1)}, u32[]{:S(2)}, u32[]{:S(2)}) %collective-permute-start.1) | collective-permute-done | bytes 4128 | tf_op jit(solution)/shard_map/ppermute | solution.py:641
  38.4 11.1 %collective-permute-start.4 = (f32[8,128]{1,0:T(8,128)S(1)}, f32[8,128]{1,0:T(8,128)S(1)}, u32[]{:S(2)}, u32[]{:S(2)}) collective-permute-start(f32[8,128]{1,0:T(8,128)S(1)} %get-tuple-element.41), channel_id=1, source_target_pairs={{0,1},{1,0},{2,3},{3,2},{4,5},{5,4},{6,7},{7,6},{8,9},{9,8},{10,11... | collective-permute-start | bytes 12296 | tf_op jit(solution)/shard_map/ppermute | solution.py:641
  49.4 0.4 shard_map.58
  49.9 1.1 collective-permute-done.4.refs_4_
  51.0 0.0 collective-permute-done.2.refs_2_
  51.0 0.0 collective-permute-done.3.refs_3_
  51.0 0.0 collective-permute-done.refs_0_
  51.0 0.0 collective-permute-done.5.refs_5_
  51.0 0.6 shard_map.59
  51.6 6.0 %collective-permute-start.6 = (f32[13,8,128]{2,1,0:T(8,128)S(1)}, f32[13,8,128]{2,1,0:T(8,128)S(1)}, u32[]{:S(2)}, u32[]{:S(2)}) collective-permute-start(f32[13,8,128]{2,1,0:T(8,128)S(1)} %get-tuple-element.47), channel_id=1, source_target_pairs={{0,896},{128,256},{256,128},{384,512},{512,384},{640,768},{768,640... | collective-permute-start | bytes 159752 | tf_op jit(solution)/shard_map/ppermute | solution.py:641
  57.6 5.1 %collective-permute-start.9 = (f32[13,8,128]{2,1,0:T(8,128)S(1)}, f32[13,8,128]{2,1,0:T(8,128)S(1)}, u32[]{:S(2)}, u32[]{:S(2)}) collective-permute-start(f32[13,8,128]{2,1,0:T(8,128)S(1)} %get-tuple-element.50), channel_id=1, source_target_pairs={{0,128},{128,0},{256,384},{384,256},{512,640},{640,512},{768,896},... | collective-permute-start | bytes 159752 | tf_op jit(solution)/shard_map/ppermute | solution.py:641
  62.8 3.0 %collective-permute-start.7 = (f32[13,4,128]{2,1,0:T(4,128)S(1)}, f32[13,4,128]{2,1,0:T(4,128)S(1)}, u32[]{:S(2)}, u32[]{:S(2)}) collective-permute-start(f32[13,4,128]{2,1,0:T(4,128)S(1)} %get-tuple-element.48), channel_id=1, source_target_pairs={{0,96},{32,64},{64,32},{96,0},{1,97},{33,65},{65,33},{97,1},{2,98}... | collective-permute-start | bytes 79880 | tf_op jit(solution)/shard_map/ppermute | solution.py:641
  65.8 2.6 %collective-permute-start.8 = (f32[13,4,128]{2,1,0:T(4,128)S(1)}, f32[13,4,128]{2,1,0:T(4,128)S(1)}, u32[]{:S(2)}, u32[]{:S(2)}) collective-permute-start(f32[13,4,128]{2,1,0:T(4,128)S(1)} %get-tuple-element.49), channel_id=1, source_target_pairs={{0,32},{32,0},{64,96},{96,64},{1,33},{33,1},{65,97},{97,65},{2,34}... | collective-permute-start | bytes 79880 | tf_op jit(solution)/shard_map/ppermute | solution.py:641
  68.4 1.3 collective-permute-done.7.yo
  69.7 1.8 %collective-permute-done.8.yp = f32[13,4,128]{2,1,0:T(4,128)S(1)} collective-permute-done((f32[13,4,128]{2,1,0:T(4,128)S(1)}, f32[13,4,128]{2,1,0:T(4,128)S(1)}, u32[]{:S(2)}, u32[]{:S(2)}) %collective-permute-start.8) | collective-permute-done | bytes 26656 | tf_op jit(solution)/shard_map/ppermute | solution.py:641
  71.6 0.0 collective-permute-done.6.xo
  71.6 0.0 collective-permute-done.9.xp
  71.6 0.3 shard_map.60
  71.8 1.9 %collective-permute-start.10 = (f32[8,128]{1,0:T(8,128)S(1)}, f32[8,128]{1,0:T(8,128)S(1)}, u32[]{:S(2)}, u32[]{:S(2)}) collective-permute-start(f32[8,128]{1,0:T(8,128)S(1)} %get-tuple-element.54), channel_id=1, source_target_pairs={{0,31},{1,2},{2,1},{3,4},{4,3},{5,6},{6,5},{7,8},{8,7},{9,10},{10,... | collective-permute-start | bytes 12296 | tf_op jit(solution)/shard_map/ppermute | solution.py:641
  73.8 10.1 %collective-permute-start.11 = (f32[8,128]{1,0:T(8,128)S(1)}, f32[8,128]{1,0:T(8,128)S(1)}, u32[]{:S(2)}, u32[]{:S(2)}) collective-permute-start(f32[8,128]{1,0:T(8,128)S(1)} %get-tuple-element.55), channel_id=1, source_target_pairs={{0,1},{1,0},{2,3},{3,2},{4,5},{5,4},{6,7},{7,6},{8,9},{9,8},{10,11... | collective-permute-start | bytes 12296 | tf_op jit(solution)/shard_map/ppermute | solution.py:641
  83.9 11.9 %all_gather.21.corner_ref = f32[8,10,128]{2,1,0:T(8,128)S(1)} all-gather(f32[2,10,128]{2,1,0:T(8,128)S(1)} %get-tuple-element.56), channel_id=1, replica_groups=mesh['gx_0'=4,'gx_1'=2,'gy'=4,'gz_0'=8,'gz_1'=4] {'gy'}, dimensions={0}, use_global_device_ids=true | all-gather | bytes 51200 | tf_op jit(solution)/shard_map/all_gather | solution.py:712
  95.8 0.0 collective-permute-done.10.zo
  95.8 0.0 collective-permute-done.11.zp
  95.8 0.5 shard_map.61
  96.3 1.8 %all-gather = f32[2,1,128]{2,1,0:T(1,128)S(1)} all-gather(f32[1,1,128]{2,1,0:T(1,128)S(1)} %bitcast.43), channel_id=1, replica_groups=mesh['gx_0'=4,'gx_1'=2,'gy'=4,'gz_0'=8,'gz_1'=4] {'gx_1'}, dimensions={0}, use_global_device_ids=true | all-gather | bytes 1536 | tf_op jit(solution)/shard_map/all_gather | solution.py:647
  98.2 9.0 %all-gather.1 = f32[4,1,128]{2,1,0:T(1,128)S(1)} all-gather(f32[1,1,128]{2,1,0:T(1,128)S(1)} %fusion.3), channel_id=1, replica_groups=mesh['gx_0'=4,'gx_1'=2,'gy'=4,'gz_0'=8,'gz_1'=4] {'gy'}, dimensions={0}, use_global_device_ids=true | all-gather | bytes 2560 | tf_op jit(solution)/shard_map/all_gather | solution.py:647
  107.2 7.0 %all-gather.2 = f32[4,1,128]{2,1,0:T(1,128)S(1)} all-gather(f32[1,1,128]{2,1,0:T(1,128)S(1)} %fusion.2), channel_id=1, replica_groups=mesh['gx_0'=4,'gx_1'=2,'gy'=4,'gz_0'=8,'gz_1'=4] {'gz_1'}, dimensions={0}, use_global_device_ids=true | all-gather | bytes 2560 | tf_op jit(solution)/shard_map/all_gather | solution.py:647
  114.2 1.9 %collective-permute-start.12 = (f32[1,128]{1,0:T(1,128)S(1)}, f32[1,128]{1,0:T(1,128)S(1)}, u32[]{:S(2)}, u32[]{:S(2)}) collective-permute-start(f32[1,128]{1,0:T(1,128)S(1)} %bitcast_select_fusion.3), channel_id=1, source_target_pairs={{0,788},{1,793},{2,798},{3,3},{4,792},{5,797},{6,2},{7,7},{8,796},... | collective-permute-start | bytes 1544 | tf_op jit(solution)/shard_map/ppermute | solution.py:665
  116.1 0.6 copy.6
  116.8 3.8 %collective-permute-done.12 = f32[1,128]{1,0:T(1,128)S(1)} collective-permute-done((f32[1,128]{1,0:T(1,128)S(1)}, f32[1,128]{1,0:T(1,128)S(1)}, u32[]{:S(2)}, u32[]{:S(2)}) %collective-permute-start.12) | collective-permute-done | bytes 544 | tf_op jit(solution)/shard_map/ppermute | solution.py:665
  120.6 1.8 %all-gather.3 = f32[2,1,128]{2,1,0:T(1,128)S(1)} all-gather(f32[1,1,128]{2,1,0:T(1,128)S(1)} %bitcast.44), channel_id=1, replica_groups=mesh['gx_0'=4,'gx_1'=2,'gy'=4,'gz_0'=8,'gz_1'=4] {'gx_1'}, dimensions={0}, use_global_device_ids=true | all-gather | bytes 1536 | tf_op jit(solution)/shard_map/all_gather | solution.py:647
  122.4 9.9 %all-gather.4 = f32[4,1,128]{2,1,0:T(1,128)S(1)} all-gather(f32[1,1,128]{2,1,0:T(1,128)S(1)} %fusion.1), channel_id=1, replica_groups=mesh['gx_0'=4,'gx_1'=2,'gy'=4,'gz_0'=8,'gz_1'=4] {'gz_1'}, dimensions={0}, use_global_device_ids=true | all-gather | bytes 2560 | tf_op jit(solution)/shard_map/all_gather | solution.py:647
  132.3 18.9 %all-gather.5 = f32[4,1,128]{2,1,0:T(1,128)S(1)} all-gather(f32[1,1,128]{2,1,0:T(1,128)S(1)} %fusion), channel_id=1, replica_groups=mesh['gx_0'=4,'gx_1'=2,'gy'=4,'gz_0'=8,'gz_1'=4] {'gx_0'}, dimensions={0}, use_global_device_ids=true | all-gather | bytes 2560 | tf_op jit(solution)/shard_map/all_gather | solution.py:647
  151.2 0.9 shard_map.62
  (12 shorter events, 0.2 us)
Async XLA Ops:
  1.7 49.3 %collective-permute-start = (f32[9,8,128]{2,1,0:T(8,128)S(1)}, f32[9,8,128]{2,1,0:T(8,128)S(1)}, u32[]{:S(2)}, u32[]{:S(2)}) collective-permute-start(f32[9,8,128]{2,1,0:T(8,128)S(1)} %get-tuple-element.37), channel_id=1, source_target_pairs={{0,896},{128,256},{256,128},{384,512},{512,384},{640,768},{768,640... | collective-permute-start | bytes 110600 | tf_op jit(solution)/shard_map/ppermute | solution.py:641
  24.1 26.9 %collective-permute-start.5 = (f32[9,8,128]{2,1,0:T(8,128)S(1)}, f32[9,8,128]{2,1,0:T(8,128)S(1)}, u32[]{:S(2)}, u32[]{:S(2)}) collective-permute-start(f32[9,8,128]{2,1,0:T(8,128)S(1)} %get-tuple-element.42), channel_id=1, source_target_pairs={{0,128},{128,0},{256,384},{384,256},{512,640},{640,512},{768,896},... | collective-permute-start | bytes 110600 | tf_op jit(solution)/shard_map/ppermute | solution.py:641
  26.0 25.0 %collective-permute-start.2 = (f32[9,4,128]{2,1,0:T(4,128)S(1)}, f32[9,4,128]{2,1,0:T(4,128)S(1)}, u32[]{:S(2)}, u32[]{:S(2)}) collective-permute-start(f32[9,4,128]{2,1,0:T(4,128)S(1)} %get-tuple-element.39), channel_id=1, source_target_pairs={{0,96},{32,64},{64,32},{96,0},{1,97},{33,65},{65,33},{97,1},{2,98}... | collective-permute-start | bytes 55304 | tf_op jit(solution)/shard_map/ppermute | solution.py:641
  30.7 20.3 %collective-permute-start.3 = (f32[9,4,128]{2,1,0:T(4,128)S(1)}, f32[9,4,128]{2,1,0:T(4,128)S(1)}, u32[]{:S(2)}, u32[]{:S(2)}) collective-permute-start(f32[9,4,128]{2,1,0:T(4,128)S(1)} %get-tuple-element.40), channel_id=1, source_target_pairs={{0,32},{32,0},{64,96},{96,64},{1,33},{33,1},{65,97},{97,65},{2,34}... | collective-permute-start | bytes 55304 | tf_op jit(solution)/shard_map/ppermute | solution.py:641
  32.9 5.5 %collective-permute-start.1 = (f32[8,128]{1,0:T(8,128)S(1)}, f32[8,128]{1,0:T(8,128)S(1)}, u32[]{:S(2)}, u32[]{:S(2)}) collective-permute-start(f32[8,128]{1,0:T(8,128)S(1)} %get-tuple-element.38), channel_id=1, source_target_pairs={{0,31},{1,2},{2,1},{3,4},{4,3},{5,6},{6,5},{7,8},{8,7},{9,10},{10,... | collective-permute-start | bytes 12296 | tf_op jit(solution)/shard_map/ppermute | solution.py:641
  38.4 12.6 %collective-permute-start.4 = (f32[8,128]{1,0:T(8,128)S(1)}, f32[8,128]{1,0:T(8,128)S(1)}, u32[]{:S(2)}, u32[]{:S(2)}) collective-permute-start(f32[8,128]{1,0:T(8,128)S(1)} %get-tuple-element.41), channel_id=1, source_target_pairs={{0,1},{1,0},{2,3},{3,2},{4,5},{5,4},{6,7},{7,6},{8,9},{9,8},{10,11... | collective-permute-start | bytes 12296 | tf_op jit(solution)/shard_map/ppermute | solution.py:641
  51.6 20.0 %collective-permute-start.6 = (f32[13,8,128]{2,1,0:T(8,128)S(1)}, f32[13,8,128]{2,1,0:T(8,128)S(1)}, u32[]{:S(2)}, u32[]{:S(2)}) collective-permute-start(f32[13,8,128]{2,1,0:T(8,128)S(1)} %get-tuple-element.47), channel_id=1, source_target_pairs={{0,896},{128,256},{256,128},{384,512},{512,384},{640,768},{768,640... | collective-permute-start | bytes 159752 | tf_op jit(solution)/shard_map/ppermute | solution.py:641
  57.6 13.9 %collective-permute-start.9 = (f32[13,8,128]{2,1,0:T(8,128)S(1)}, f32[13,8,128]{2,1,0:T(8,128)S(1)}, u32[]{:S(2)}, u32[]{:S(2)}) collective-permute-start(f32[13,8,128]{2,1,0:T(8,128)S(1)} %get-tuple-element.50), channel_id=1, source_target_pairs={{0,128},{128,0},{256,384},{384,256},{512,640},{640,512},{768,896},... | collective-permute-start | bytes 159752 | tf_op jit(solution)/shard_map/ppermute | solution.py:641
  62.8 7.0 %collective-permute-start.7 = (f32[13,4,128]{2,1,0:T(4,128)S(1)}, f32[13,4,128]{2,1,0:T(4,128)S(1)}, u32[]{:S(2)}, u32[]{:S(2)}) collective-permute-start(f32[13,4,128]{2,1,0:T(4,128)S(1)} %get-tuple-element.48), channel_id=1, source_target_pairs={{0,96},{32,64},{64,32},{96,0},{1,97},{33,65},{65,33},{97,1},{2,98}... | collective-permute-start | bytes 79880 | tf_op jit(solution)/shard_map/ppermute | solution.py:641
  65.8 5.7 %collective-permute-start.8 = (f32[13,4,128]{2,1,0:T(4,128)S(1)}, f32[13,4,128]{2,1,0:T(4,128)S(1)}, u32[]{:S(2)}, u32[]{:S(2)}) collective-permute-start(f32[13,4,128]{2,1,0:T(4,128)S(1)} %get-tuple-element.49), channel_id=1, source_target_pairs={{0,32},{32,0},{64,96},{96,64},{1,33},{33,1},{65,97},{97,65},{2,34}... | collective-permute-start | bytes 79880 | tf_op jit(solution)/shard_map/ppermute | solution.py:641
  71.8 24.0 %collective-permute-start.10 = (f32[8,128]{1,0:T(8,128)S(1)}, f32[8,128]{1,0:T(8,128)S(1)}, u32[]{:S(2)}, u32[]{:S(2)}) collective-permute-start(f32[8,128]{1,0:T(8,128)S(1)} %get-tuple-element.54), channel_id=1, source_target_pairs={{0,31},{1,2},{2,1},{3,4},{4,3},{5,6},{6,5},{7,8},{8,7},{9,10},{10,... | collective-permute-start | bytes 12296 | tf_op jit(solution)/shard_map/ppermute | solution.py:641
  73.8 22.0 %collective-permute-start.11 = (f32[8,128]{1,0:T(8,128)S(1)}, f32[8,128]{1,0:T(8,128)S(1)}, u32[]{:S(2)}, u32[]{:S(2)}) collective-permute-start(f32[8,128]{1,0:T(8,128)S(1)} %get-tuple-element.55), channel_id=1, source_target_pairs={{0,1},{1,0},{2,3},{3,2},{4,5},{5,4},{6,7},{7,6},{8,9},{9,8},{10,11... | collective-permute-start | bytes 12296 | tf_op jit(solution)/shard_map/ppermute | solution.py:641
  114.2 6.4 %collective-permute-start.12 = (f32[1,128]{1,0:T(1,128)S(1)}, f32[1,128]{1,0:T(1,128)S(1)}, u32[]{:S(2)}, u32[]{:S(2)}) collective-permute-start(f32[1,128]{1,0:T(1,128)S(1)} %bitcast_select_fusion.3), channel_id=1, source_target_pairs={{0,788},{1,793},{2,798},{3,3},{4,792},{5,797},{6,2},{7,7},{8,796},... | collective-permute-start | bytes 1544 | tf_op jit(solution)/shard_map/ppermute | solution.py:665

commit v3 on v1

--- a/solution.py
+++ b/solution.py
@@ -652,11 +652,7 @@
     pairs = []
     for at in np.ndindex(*sizes):
         a, core, b, c, e = at
-        half = sizes[4] // 2
-        step = e - (half - 1)
-        if core:
-            step += half if step > 0 else -half
-        place = (a * sizes[3] + c + step) % ring
+        place = (a * sizes[3] + c + core * sizes[4] + e - (sizes[3] // 2 - 1)) % ring
         to = (place // sizes[3], core, b, place % sizes[3], e)
         pairs.append(
             (int(np.ravel_multi_index(at, sizes)), int(np.ravel_multi_index(to, sizes)))
@@ -665,10 +661,10 @@
 
 
 def over_all(stat):
-    for axis in ("gx_1", "gy", "gz_1"):
+    for axis in ("gx_0", "gx_1", "gy", "gz_1"):
         stat = gather(stat, axis)
     stat = spread(stat)
-    for axis in ("gx_1", "gz_1", "gx_0"):
+    for axis in ("gx_1", "gz_1"):
         stat = gather(stat, axis)
     return stat
 

time: 150 us -> 149 us (level)
  the two profiles are of different devices: /device:TPU:8 before, /device:TPU:72 now
where the time goes in v3:
time: 149 us; the launch traced here: 148 us
  starting transfers between devices  83.2 us (56%)
  blocking collectives  51.3 us (34%)
  waiting for transfers between devices  8.5 us (6%)
  Pallas kernels  3.8 us (3%)
    ppermute x14, starting transfers between devices, exchange(): lax.ppermute(message, axis, [(a, partner(a, size)) for a in range(size)])  69.9 us
    all_gather x6, blocking collectives, gather(): every = lax.all_gather(stat, axis, tiled=True)  51.3 us
    ppermute x1, starting transfers between devices, spread(): return lax.ppermute(stat, names, pairs)  13.3 us
    ppermute x14, waiting for transfers between devices, exchange(): lax.ppermute(message, axis, [(a, partner(a, size)) for a in range(size)])  7.86 us
    pallas_call x6, Pallas kernels, run(): pl.pallas_call(kernel, in_specs=[pl.BlockSpec(memory_space=pltpu.VMEM)] *...  3.8 us
  transfers between devices with their start and end apart: 15, of which 6 were waited for; matrix products, arithmetic and copies ran while one was open for 0% of the time, Pallas kernels for 0%

profile of v3, /device:TPU:72, one launch (start us, length us, event | category | flops | bytes accessed | tf_op | source)
XLA Modules:
  0.0 148.4 jit_solution(2812856758394496969)
XLA Ops:
  0.6 1.0 shard_map.57
  1.7 20.6 %collective-permute-start = (f32[9,8,128]{2,1,0:T(8,128)S(1)}, f32[9,8,128]{2,1,0:T(8,128)S(1)}, u32[]{:S(2)}, u32[]{:S(2)}) collective-permute-start(f32[9,8,128]{2,1,0:T(8,128)S(1)} %get-tuple-element.38), channel_id=1, source_target_pairs={{0,896},{128,256},{256,128},{384,512},{512,384},{640,768},{768,640... | collective-permute-start | bytes 110600 | tf_op jit(solution)/shard_map/ppermute | solution.py:636
  22.3 1.9 %collective-permute-start.5 = (f32[9,8,128]{2,1,0:T(8,128)S(1)}, f32[9,8,128]{2,1,0:T(8,128)S(1)}, u32[]{:S(2)}, u32[]{:S(2)}) collective-permute-start(f32[9,8,128]{2,1,0:T(8,128)S(1)} %get-tuple-element.43), channel_id=1, source_target_pairs={{0,128},{128,0},{256,384},{384,256},{512,640},{640,512},{768,896},... | collective-permute-start | bytes 110600 | tf_op jit(solution)/shard_map/ppermute | solution.py:636
  24.2 4.7 %collective-permute-start.2 = (f32[9,4,128]{2,1,0:T(4,128)S(1)}, f32[9,4,128]{2,1,0:T(4,128)S(1)}, u32[]{:S(2)}, u32[]{:S(2)}) collective-permute-start(f32[9,4,128]{2,1,0:T(4,128)S(1)} %get-tuple-element.40), channel_id=1, source_target_pairs={{0,96},{32,64},{64,32},{96,0},{1,97},{33,65},{65,33},{97,1},{2,98}... | collective-permute-start | bytes 55304 | tf_op jit(solution)/shard_map/ppermute | solution.py:636
  28.9 2.1 %collective-permute-start.3 = (f32[9,4,128]{2,1,0:T(4,128)S(1)}, f32[9,4,128]{2,1,0:T(4,128)S(1)}, u32[]{:S(2)}, u32[]{:S(2)}) collective-permute-start(f32[9,4,128]{2,1,0:T(4,128)S(1)} %get-tuple-element.41), channel_id=1, source_target_pairs={{0,32},{32,0},{64,96},{96,64},{1,33},{33,1},{65,97},{97,65},{2,34}... | collective-permute-start | bytes 55304 | tf_op jit(solution)/shard_map/ppermute | solution.py:636
  31.1 3.5 %collective-permute-start.1 = (f32[8,128]{1,0:T(8,128)S(1)}, f32[8,128]{1,0:T(8,128)S(1)}, u32[]{:S(2)}, u32[]{:S(2)}) collective-permute-start(f32[8,128]{1,0:T(8,128)S(1)} %get-tuple-element.39), channel_id=1, source_target_pairs={{0,31},{1,2},{2,1},{3,4},{4,3},{5,6},{6,5},{7,8},{8,7},{9,10},{10,... | collective-permute-start | bytes 12296 | tf_op jit(solution)/shard_map/ppermute | solution.py:636
  34.6 2.0 %collective-permute-done.1.refs_1_ = f32[8,128]{1,0:T(8,128)S(1)} collective-permute-done((f32[8,128]{1,0:T(8,128)S(1)}, f32[8,128]{1,0:T(8,128)S(1)}, u32[]{:S(2)}, u32[]{:S(2)}) %collective-permute-start.1) | collective-permute-done | bytes 4128 | tf_op jit(solution)/shard_map/ppermute | solution.py:636
  36.6 4.5 %collective-permute-start.4 = (f32[8,128]{1,0:T(8,128)S(1)}, f32[8,128]{1,0:T(8,128)S(1)}, u32[]{:S(2)}, u32[]{:S(2)}) collective-permute-start(f32[8,128]{1,0:T(8,128)S(1)} %get-tuple-element.42), channel_id=1, source_target_pairs={{0,1},{1,0},{2,3},{3,2},{4,5},{5,4},{6,7},{7,6},{8,9},{9,8},{10,11... | collective-permute-start | bytes 12296 | tf_op jit(solution)/shard_map/ppermute | solution.py:636
  41.0 0.4 shard_map.58
  41.5 1.1 collective-permute-done.4.refs_4_
  42.6 0.0 collective-permute-done.2.refs_2_
  42.6 0.0 collective-permute-done.3.refs_3_
  42.6 0.0 collective-permute-done.refs_0_
  42.6 0.0 collective-permute-done.5.refs_5_
  42.6 0.6 shard_map.59
  43.2 6.0 %collective-permute-start.6 = (f32[13,8,128]{2,1,0:T(8,128)S(1)}, f32[13,8,128]{2,1,0:T(8,128)S(1)}, u32[]{:S(2)}, u32[]{:S(2)}) collective-permute-start(f32[13,8,128]{2,1,0:T(8,128)S(1)} %get-tuple-element.48), channel_id=1, source_target_pairs={{0,896},{128,256},{256,128},{384,512},{512,384},{640,768},{768,640... | collective-permute-start | bytes 159752 | tf_op jit(solution)/shard_map/ppermute | solution.py:636
  49.2 5.1 %collective-permute-start.9 = (f32[13,8,128]{2,1,0:T(8,128)S(1)}, f32[13,8,128]{2,1,0:T(8,128)S(1)}, u32[]{:S(2)}, u32[]{:S(2)}) collective-permute-start(f32[13,8,128]{2,1,0:T(8,128)S(1)} %get-tuple-element.51), channel_id=1, source_target_pairs={{0,128},{128,0},{256,384},{384,256},{512,640},{640,512},{768,896},... | collective-permute-start | bytes 159752 | tf_op jit(solution)/shard_map/ppermute | solution.py:636
  54.4 3.0 %collective-permute-start.7 = (f32[13,4,128]{2,1,0:T(4,128)S(1)}, f32[13,4,128]{2,1,0:T(4,128)S(1)}, u32[]{:S(2)}, u32[]{:S(2)}) collective-permute-start(f32[13,4,128]{2,1,0:T(4,128)S(1)} %get-tuple-element.49), channel_id=1, source_target_pairs={{0,96},{32,64},{64,32},{96,0},{1,97},{33,65},{65,33},{97,1},{2,98}... | collective-permute-start | bytes 79880 | tf_op jit(solution)/shard_map/ppermute | solution.py:636
  57.4 2.6 %collective-permute-start.8 = (f32[13,4,128]{2,1,0:T(4,128)S(1)}, f32[13,4,128]{2,1,0:T(4,128)S(1)}, u32[]{:S(2)}, u32[]{:S(2)}) collective-permute-start(f32[13,4,128]{2,1,0:T(4,128)S(1)} %get-tuple-element.50), channel_id=1, source_target_pairs={{0,32},{32,0},{64,96},{96,64},{1,33},{33,1},{65,97},{97,65},{2,34}... | collective-permute-start | bytes 79880 | tf_op jit(solution)/shard_map/ppermute | solution.py:636
  60.0 1.3 collective-permute-done.7.yo
  61.3 1.8 %collective-permute-done.8.yp = f32[13,4,128]{2,1,0:T(4,128)S(1)} collective-permute-done((f32[13,4,128]{2,1,0:T(4,128)S(1)}, f32[13,4,128]{2,1,0:T(4,128)S(1)}, u32[]{:S(2)}, u32[]{:S(2)}) %collective-permute-start.8) | collective-permute-done | bytes 26656 | tf_op jit(solution)/shard_map/ppermute | solution.py:636
  63.2 0.0 collective-permute-done.6.xo
  63.2 0.0 collective-permute-done.9.xp
  63.2 0.3 shard_map.60
  63.4 4.0 %collective-permute-start.11 = (f32[10,128]{1,0:T(8,128)S(1)}, f32[10,128]{1,0:T(8,128)S(1)}, u32[]{:S(2)}, u32[]{:S(2)}) collective-permute-start(f32[10,128]{1,0:T(8,128)S(1)} %get-tuple-element.56), channel_id=1, source_target_pairs={{0,96},{32,64},{64,32},{96,0},{1,97},{33,65},{65,33},{97,1},{2,98}... | collective-permute-start | bytes 15368 | tf_op jit(solution)/shard_map/ppermute | solution.py:636
  67.5 2.5 %collective-permute-start.12 = (f32[10,128]{1,0:T(8,128)S(1)}, f32[10,128]{1,0:T(8,128)S(1)}, u32[]{:S(2)}, u32[]{:S(2)}) collective-permute-start(f32[10,128]{1,0:T(8,128)S(1)} %get-tuple-element.57), channel_id=1, source_target_pairs={{0,32},{32,0},{64,96},{96,64},{1,33},{33,1},{65,97},{97,65},{2,34}... | collective-permute-start | bytes 15368 | tf_op jit(solution)/shard_map/ppermute | solution.py:636
  70.0 4.3 %collective-permute-start.10 = (f32[8,128]{1,0:T(8,128)S(1)}, f32[8,128]{1,0:T(8,128)S(1)}, u32[]{:S(2)}, u32[]{:S(2)}) collective-permute-start(f32[8,128]{1,0:T(8,128)S(1)} %get-tuple-element.55), channel_id=1, source_target_pairs={{0,31},{1,2},{2,1},{3,4},{4,3},{5,6},{6,5},{7,8},{8,7},{9,10},{10,... | collective-permute-start | bytes 12296 | tf_op jit(solution)/shard_map/ppermute | solution.py:636
  74.3 5.0 %collective-permute-start.13 = (f32[8,128]{1,0:T(8,128)S(1)}, f32[8,128]{1,0:T(8,128)S(1)}, u32[]{:S(2)}, u32[]{:S(2)}) collective-permute-start(f32[8,128]{1,0:T(8,128)S(1)} %get-tuple-element.58), channel_id=1, source_target_pairs={{0,1},{1,0},{2,3},{3,2},{4,5},{5,4},{6,7},{7,6},{8,9},{9,8},{10,11... | collective-permute-start | bytes 12296 | tf_op jit(solution)/shard_map/ppermute | solution.py:636
  79.3 0.0 collective-permute-done.10.zo
  79.3 1.6 %collective-permute-done.13.zp = f32[8,128]{1,0:T(8,128)S(1)} collective-permute-done((f32[8,128]{1,0:T(8,128)S(1)}, f32[8,128]{1,0:T(8,128)S(1)}, u32[]{:S(2)}, u32[]{:S(2)}) %collective-permute-start.13) | collective-permute-done | bytes 4128 | tf_op jit(solution)/shard_map/ppermute | solution.py:636
  80.8 0.0 collective-permute-done.11.eo
  80.8 0.0 collective-permute-done.12.ep
  80.8 0.5 shard_map.61
  81.4 18.7 %all-gather = f32[4,1,128]{2,1,0:T(1,128)S(1)} all-gather(f32[1,1,128]{2,1,0:T(1,128)S(1)} %bitcast.43), channel_id=1, replica_groups=mesh['gx_0'=4,'gx_1'=2,'gy'=4,'gz_0'=8,'gz_1'=4] {'gx_0'}, dimensions={0}, use_global_device_ids=true | all-gather | bytes 2560 | tf_op jit(solution)/shard_map/all_gather | solution.py:642
  100.1 1.8 %all-gather.1 = f32[2,1,128]{2,1,0:T(1,128)S(1)} all-gather(f32[1,1,128]{2,1,0:T(1,128)S(1)} %fusion.3), channel_id=1, replica_groups=mesh['gx_0'=4,'gx_1'=2,'gy'=4,'gz_0'=8,'gz_1'=4] {'gx_1'}, dimensions={0}, use_global_device_ids=true | all-gather | bytes 1536 | tf_op jit(solution)/shard_map/all_gather | solution.py:642
  101.9 8.4 %all-gather.2 = f32[4,1,128]{2,1,0:T(1,128)S(1)} all-gather(f32[1,1,128]{2,1,0:T(1,128)S(1)} %fusion.2), channel_id=1, replica_groups=mesh['gx_0'=4,'gx_1'=2,'gy'=4,'gz_0'=8,'gz_1'=4] {'gy'}, dimensions={0}, use_global_device_ids=true | all-gather | bytes 2560 | tf_op jit(solution)/shard_map/all_gather | solution.py:642
  110.3 9.0 %all-gather.3 = f32[4,1,128]{2,1,0:T(1,128)S(1)} all-gather(f32[1,1,128]{2,1,0:T(1,128)S(1)} %fusion.1), channel_id=1, replica_groups=mesh['gx_0'=4,'gx_1'=2,'gy'=4,'gz_0'=8,'gz_1'=4] {'gz_1'}, dimensions={0}, use_global_device_ids=true | all-gather | bytes 2560 | tf_op jit(solution)/shard_map/all_gather | solution.py:642
  119.3 13.3 %collective-permute-start.14 = (f32[1,128]{1,0:T(1,128)S(1)}, f32[1,128]{1,0:T(1,128)S(1)}, u32[]{:S(2)}, u32[]{:S(2)}) collective-permute-start(f32[1,128]{1,0:T(1,128)S(1)} %bitcast_select_fusion.2), channel_id=1, source_target_pairs={{0,788},{1,793},{2,798},{3,3},{4,792},{5,797},{6,2},{7,7},{8,796},... | collective-permute-start | bytes 1544 | tf_op jit(solution)/shard_map/ppermute | solution.py:660
  132.7 0.6 copy.6
  133.3 0.6 collective-permute-done.14
  133.9 1.8 %all-gather.4 = f32[2,1,128]{2,1,0:T(1,128)S(1)} all-gather(f32[1,1,128]{2,1,0:T(1,128)S(1)} %bitcast.44), channel_id=1, replica_groups=mesh['gx_0'=4,'gx_1'=2,'gy'=4,'gz_0'=8,'gz_1'=4] {'gx_1'}, dimensions={0}, use_global_device_ids=true | all-gather | bytes 1536 | tf_op jit(solution)/shard_map/all_gather | solution.py:642
  135.8 11.6 %all-gather.5 = f32[4,1,128]{2,1,0:T(1,128)S(1)} all-gather(f32[1,1,128]{2,1,0:T(1,128)S(1)} %fusion), channel_id=1, replica_groups=mesh['gx_0'=4,'gx_1'=2,'gy'=4,'gz_0'=8,'gz_1'=4] {'gz_1'}, dimensions={0}, use_global_device_ids=true | all-gather | bytes 2560 | tf_op jit(solution)/shard_map/all_gather | solution.py:642
  147.4 0.9 shard_map.62
  (12 shorter events, 0.2 us)
Async XLA Ops:
  1.7 40.9 %collective-permute-start = (f32[9,8,128]{2,1,0:T(8,128)S(1)}, f32[9,8,128]{2,1,0:T(8,128)S(1)}, u32[]{:S(2)}, u32[]{:S(2)}) collective-permute-start(f32[9,8,128]{2,1,0:T(8,128)S(1)} %get-tuple-element.38), channel_id=1, source_target_pairs={{0,896},{128,256},{256,128},{384,512},{512,384},{640,768},{768,640... | collective-permute-start | bytes 110600 | tf_op jit(solution)/shard_map/ppermute | solution.py:636
  22.3 20.3 %collective-permute-start.5 = (f32[9,8,128]{2,1,0:T(8,128)S(1)}, f32[9,8,128]{2,1,0:T(8,128)S(1)}, u32[]{:S(2)}, u32[]{:S(2)}) collective-permute-start(f32[9,8,128]{2,1,0:T(8,128)S(1)} %get-tuple-element.43), channel_id=1, source_target_pairs={{0,128},{128,0},{256,384},{384,256},{512,640},{640,512},{768,896},... | collective-permute-start | bytes 110600 | tf_op jit(solution)/shard_map/ppermute | solution.py:636
  24.2 18.4 %collective-permute-start.2 = (f32[9,4,128]{2,1,0:T(4,128)S(1)}, f32[9,4,128]{2,1,0:T(4,128)S(1)}, u32[]{:S(2)}, u32[]{:S(2)}) collective-permute-start(f32[9,4,128]{2,1,0:T(4,128)S(1)} %get-tuple-element.40), channel_id=1, source_target_pairs={{0,96},{32,64},{64,32},{96,0},{1,97},{33,65},{65,33},{97,1},{2,98}... | collective-permute-start | bytes 55304 | tf_op jit(solution)/shard_map/ppermute | solution.py:636
  28.9 13.7 %collective-permute-start.3 = (f32[9,4,128]{2,1,0:T(4,128)S(1)}, f32[9,4,128]{2,1,0:T(4,128)S(1)}, u32[]{:S(2)}, u32[]{:S(2)}) collective-permute-start(f32[9,4,128]{2,1,0:T(4,128)S(1)} %get-tuple-element.41), channel_id=1, source_target_pairs={{0,32},{32,0},{64,96},{96,64},{1,33},{33,1},{65,97},{97,65},{2,34}... | collective-permute-start | bytes 55304 | tf_op jit(solution)/shard_map/ppermute | solution.py:636
  31.1 5.5 %collective-permute-start.1 = (f32[8,128]{1,0:T(8,128)S(1)}, f32[8,128]{1,0:T(8,128)S(1)}, u32[]{:S(2)}, u32[]{:S(2)}) collective-permute-start(f32[8,128]{1,0:T(8,128)S(1)} %get-tuple-element.39), channel_id=1, source_target_pairs={{0,31},{1,2},{2,1},{3,4},{4,3},{5,6},{6,5},{7,8},{8,7},{9,10},{10,... | collective-permute-start | bytes 12296 | tf_op jit(solution)/shard_map/ppermute | solution.py:636
  36.6 6.0 %collective-permute-start.4 = (f32[8,128]{1,0:T(8,128)S(1)}, f32[8,128]{1,0:T(8,128)S(1)}, u32[]{:S(2)}, u32[]{:S(2)}) collective-permute-start(f32[8,128]{1,0:T(8,128)S(1)} %get-tuple-element.42), channel_id=1, source_target_pairs={{0,1},{1,0},{2,3},{3,2},{4,5},{5,4},{6,7},{7,6},{8,9},{9,8},{10,11... | collective-permute-start | bytes 12296 | tf_op jit(solution)/shard_map/ppermute | solution.py:636
  43.2 20.0 %collective-permute-start.6 = (f32[13,8,128]{2,1,0:T(8,128)S(1)}, f32[13,8,128]{2,1,0:T(8,128)S(1)}, u32[]{:S(2)}, u32[]{:S(2)}) collective-permute-start(f32[13,8,128]{2,1,0:T(8,128)S(1)} %get-tuple-element.48), channel_id=1, source_target_pairs={{0,896},{128,256},{256,128},{384,512},{512,384},{640,768},{768,640... | collective-permute-start | bytes 159752 | tf_op jit(solution)/shard_map/ppermute | solution.py:636
  49.2 13.9 %collective-permute-start.9 = (f32[13,8,128]{2,1,0:T(8,128)S(1)}, f32[13,8,128]{2,1,0:T(8,128)S(1)}, u32[]{:S(2)}, u32[]{:S(2)}) collective-permute-start(f32[13,8,128]{2,1,0:T(8,128)S(1)} %get-tuple-element.51), channel_id=1, source_target_pairs={{0,128},{128,0},{256,384},{384,256},{512,640},{640,512},{768,896},... | collective-permute-start | bytes 159752 | tf_op jit(solution)/shard_map/ppermute | solution.py:636
  54.4 7.0 %collective-permute-start.7 = (f32[13,4,128]{2,1,0:T(4,128)S(1)}, f32[13,4,128]{2,1,0:T(4,128)S(1)}, u32[]{:S(2)}, u32[]{:S(2)}) collective-permute-start(f32[13,4,128]{2,1,0:T(4,128)S(1)} %get-tuple-element.49), channel_id=1, source_target_pairs={{0,96},{32,64},{64,32},{96,0},{1,97},{33,65},{65,33},{97,1},{2,98}... | collective-permute-start | bytes 79880 | tf_op jit(solution)/shard_map/ppermute | solution.py:636
  57.4 5.7 %collective-permute-start.8 = (f32[13,4,128]{2,1,0:T(4,128)S(1)}, f32[13,4,128]{2,1,0:T(4,128)S(1)}, u32[]{:S(2)}, u32[]{:S(2)}) collective-permute-start(f32[13,4,128]{2,1,0:T(4,128)S(1)} %get-tuple-element.50), channel_id=1, source_target_pairs={{0,32},{32,0},{64,96},{96,64},{1,33},{33,1},{65,97},{97,65},{2,34}... | collective-permute-start | bytes 79880 | tf_op jit(solution)/shard_map/ppermute | solution.py:636
  63.4 17.4 %collective-permute-start.11 = (f32[10,128]{1,0:T(8,128)S(1)}, f32[10,128]{1,0:T(8,128)S(1)}, u32[]{:S(2)}, u32[]{:S(2)}) collective-permute-start(f32[10,128]{1,0:T(8,128)S(1)} %get-tuple-element.56), channel_id=1, source_target_pairs={{0,96},{32,64},{64,32},{96,0},{1,97},{33,65},{65,33},{97,1},{2,98}... | collective-permute-start | bytes 15368 | tf_op jit(solution)/shard_map/ppermute | solution.py:636
  67.5 13.4 %collective-permute-start.12 = (f32[10,128]{1,0:T(8,128)S(1)}, f32[10,128]{1,0:T(8,128)S(1)}, u32[]{:S(2)}, u32[]{:S(2)}) collective-permute-start(f32[10,128]{1,0:T(8,128)S(1)} %get-tuple-element.57), channel_id=1, source_target_pairs={{0,32},{32,0},{64,96},{96,64},{1,33},{33,1},{65,97},{97,65},{2,34}... | collective-permute-start | bytes 15368 | tf_op jit(solution)/shard_map/ppermute | solution.py:636
  70.0 9.3 %collective-permute-start.10 = (f32[8,128]{1,0:T(8,128)S(1)}, f32[8,128]{1,0:T(8,128)S(1)}, u32[]{:S(2)}, u32[]{:S(2)}) collective-permute-start(f32[8,128]{1,0:T(8,128)S(1)} %get-tuple-element.55), channel_id=1, source_target_pairs={{0,31},{1,2},{2,1},{3,4},{4,3},{5,6},{6,5},{7,8},{8,7},{9,10},{10,... | collective-permute-start | bytes 12296 | tf_op jit(solution)/shard_map/ppermute | solution.py:636
  74.3 6.5 %collective-permute-start.13 = (f32[8,128]{1,0:T(8,128)S(1)}, f32[8,128]{1,0:T(8,128)S(1)}, u32[]{:S(2)}, u32[]{:S(2)}) collective-permute-start(f32[8,128]{1,0:T(8,128)S(1)} %get-tuple-element.58), channel_id=1, source_target_pairs={{0,1},{1,0},{2,3},{3,2},{4,5},{5,4},{6,7},{7,6},{8,9},{9,8},{10,11... | collective-permute-start | bytes 12296 | tf_op jit(solution)/shard_map/ppermute | solution.py:636
  119.3 14.6 %collective-permute-start.14 = (f32[1,128]{1,0:T(1,128)S(1)}, f32[1,128]{1,0:T(1,128)S(1)}, u32[]{:S(2)}, u32[]{:S(2)}) collective-permute-start(f32[1,128]{1,0:T(1,128)S(1)} %bitcast_select_fusion.2), channel_id=1, source_target_pairs={{0,788},{1,793},{2,798},{3,3},{4,792},{5,797},{6,2},{7,7},{8,796},... | collective-permute-start | bytes 1544 | tf_op jit(solution)/shard_map/ppermute | solution.py:660

commit v4 on v3

--- a/solution.py
+++ b/solution.py
@@ -431,7 +431,7 @@
     return [field[first + c][x] for c in range(count)]
 
 
-def join_kernel(f1_ref, f2_ref, xo, yo, yp, xp, f2_out, side_ref, row_ref, zo, eo, ep, zp):
+def join_kernel(f1_ref, f2_ref, xo, yo, yp, xp, f2_out, side_ref, row_ref, eo, zo, ep, zp):
     even = is_even()
     y = Line(0)
     f1, f2 = (load(f1_ref), load(f2_ref))
@@ -489,7 +489,7 @@
 
 
 def last_kernel(
-    u_ref, rate_ref, fast_ref, f1_ref, f2_ref, side_ref, row_ref, zo, eo, ep, zp, next_ref, stat_ref
+    u_ref, rate_ref, fast_ref, f1_ref, f2_ref, side_ref, row_ref, eo, zo, ep, zp, next_ref, stat_ref
 ):
     even = is_even()
     y, z = (Line(0), Line(1))
@@ -617,15 +617,15 @@
 
 ROUTES = {
     "state": (
+        ("gy", other_of),
         (GX, other_of),
         (GZ, other_of),
-        ("gy", other_of),
         ("gy", pair_of),
         (GZ, pair_of),
         (GX, pair_of),
     ),
     "second": ((GX, other_of), ("gy", other_of), ("gy", pair_of), (GX, pair_of)),
-    "third": ((GZ, other_of), ("gy", other_of), ("gy", pair_of), (GZ, pair_of)),
+    "third": (("gy", other_of), (GZ, other_of), ("gy", pair_of), (GZ, pair_of)),
 }
 
 
@@ -689,7 +689,9 @@
         10**5,
         False,
     )(u, g)
-    received = exchange(messages, "state")
+    xo, zo, yo, *rest = messages
+    yo, xo, zo, *rest = exchange([yo, xo, zo, *rest], "state")
+    received = [xo, zo, yo, *rest]
     vol, alpha, fast = call(volume_kernel, [shape(5, *full), tile, tile], 10**7)(u)
     planes, rows = (shape(13, NY, NZ), shape(13, NX, NZ))
     rate, f1, f2, *messages = call(
@@ -701,7 +703,7 @@
     corners = shape(10, NZ)
     f2, sides, rows, *messages = call(
         join_kernel,
-        [shape(8, *full), shape(2, 13, NY, NZ), shape(13, *full), tile, corners, corners, tile],
+        [shape(8, *full), shape(2, 13, NY, NZ), shape(13, *full), corners, tile, corners, tile],
         10**6,
     )(f1, f2, *received)
     received = exchange(messages, "third")

time: 149 us -> 149 us (level)
  no operation moved by 1% of the time
where the time goes in v4:
time: 149 us; the launch traced here: 148 us
  starting transfers between devices  83.2 us (56%)
  blocking collectives  51.3 us (34%)
  waiting for transfers between devices  8.5 us (6%)
  Pallas kernels  3.8 us (3%)
    ppermute x14, starting transfers between devices, exchange(): lax.ppermute(message, axis, [(a, partner(a, size)) for a in range(size)])  69.9 us
    all_gather x6, blocking collectives, gather(): every = lax.all_gather(stat, axis, tiled=True)  51.3 us
    ppermute x1, starting transfers between devices, spread(): return lax.ppermute(stat, names, pairs)  13.3 us
    ppermute x14, waiting for transfers between devices, exchange(): lax.ppermute(message, axis, [(a, partner(a, size)) for a in range(size)])  7.86 us
    pallas_call x6, Pallas kernels, run(): pl.pallas_call(kernel, in_specs=[pl.BlockSpec(memory_space=pltpu.VMEM)] *...  3.8 us
  transfers between devices with their start and end apart: 15, of which 6 were waited for; matrix products, arithmetic and copies ran while one was open for 0% of the time, Pallas kernels for 0%

profile of v4, /device:TPU:72, one launch (start us, length us, event | category | flops | bytes accessed | tf_op | source)
XLA Modules:
  0.0 148.4 jit_solution(8618780360428540600)
XLA Ops:
  0.6 1.0 shard_map.57
  1.7 20.6 %collective-permute-start = (f32[9,8,128]{2,1,0:T(8,128)S(1)}, f32[9,8,128]{2,1,0:T(8,128)S(1)}, u32[]{:S(2)}, u32[]{:S(2)}) collective-permute-start(f32[9,8,128]{2,1,0:T(8,128)S(1)} %get-tuple-element.38), channel_id=1, source_target_pairs={{0,896},{128,256},{256,128},{384,512},{512,384},{640,768},{768,640... | collective-permute-start | bytes 110600 | tf_op jit(solution)/shard_map/ppermute | solution.py:636
  22.3 1.9 %collective-permute-start.5 = (f32[9,8,128]{2,1,0:T(8,128)S(1)}, f32[9,8,128]{2,1,0:T(8,128)S(1)}, u32[]{:S(2)}, u32[]{:S(2)}) collective-permute-start(f32[9,8,128]{2,1,0:T(8,128)S(1)} %get-tuple-element.43), channel_id=1, source_target_pairs={{0,128},{128,0},{256,384},{384,256},{512,640},{640,512},{768,896},... | collective-permute-start | bytes 110600 | tf_op jit(solution)/shard_map/ppermute | solution.py:636
  24.2 4.7 %collective-permute-start.2 = (f32[9,4,128]{2,1,0:T(4,128)S(1)}, f32[9,4,128]{2,1,0:T(4,128)S(1)}, u32[]{:S(2)}, u32[]{:S(2)}) collective-permute-start(f32[9,4,128]{2,1,0:T(4,128)S(1)} %get-tuple-element.40), channel_id=1, source_target_pairs={{0,96},{32,64},{64,32},{96,0},{1,97},{33,65},{65,33},{97,1},{2,98}... | collective-permute-start | bytes 55304 | tf_op jit(solution)/shard_map/ppermute | solution.py:636
  28.9 2.1 %collective-permute-start.3 = (f32[9,4,128]{2,1,0:T(4,128)S(1)}, f32[9,4,128]{2,1,0:T(4,128)S(1)}, u32[]{:S(2)}, u32[]{:S(2)}) collective-permute-start(f32[9,4,128]{2,1,0:T(4,128)S(1)} %get-tuple-element.41), channel_id=1, source_target_pairs={{0,32},{32,0},{64,96},{96,64},{1,33},{33,1},{65,97},{97,65},{2,34}... | collective-permute-start | bytes 55304 | tf_op jit(solution)/shard_map/ppermute | solution.py:636
  31.1 3.5 %collective-permute-start.1 = (f32[8,128]{1,0:T(8,128)S(1)}, f32[8,128]{1,0:T(8,128)S(1)}, u32[]{:S(2)}, u32[]{:S(2)}) collective-permute-start(f32[8,128]{1,0:T(8,128)S(1)} %get-tuple-element.39), channel_id=1, source_target_pairs={{0,31},{1,2},{2,1},{3,4},{4,3},{5,6},{6,5},{7,8},{8,7},{9,10},{10,... | collective-permute-start | bytes 12296 | tf_op jit(solution)/shard_map/ppermute | solution.py:636
  34.6 2.0 %collective-permute-done.1.refs_1_ = f32[8,128]{1,0:T(8,128)S(1)} collective-permute-done((f32[8,128]{1,0:T(8,128)S(1)}, f32[8,128]{1,0:T(8,128)S(1)}, u32[]{:S(2)}, u32[]{:S(2)}) %collective-permute-start.1) | collective-permute-done | bytes 4128 | tf_op jit(solution)/shard_map/ppermute | solution.py:636
  36.6 4.5 %collective-permute-start.4 = (f32[8,128]{1,0:T(8,128)S(1)}, f32[8,128]{1,0:T(8,128)S(1)}, u32[]{:S(2)}, u32[]{:S(2)}) collective-permute-start(f32[8,128]{1,0:T(8,128)S(1)} %get-tuple-element.42), channel_id=1, source_target_pairs={{0,1},{1,0},{2,3},{3,2},{4,5},{5,4},{6,7},{7,6},{8,9},{9,8},{10,11... | collective-permute-start | bytes 12296 | tf_op jit(solution)/shard_map/ppermute | solution.py:636
  41.0 0.4 shard_map.58
  41.5 1.1 collective-permute-done.4.refs_4_
  42.6 0.0 collective-permute-done.2.refs_2_
  42.6 0.0 collective-permute-done.3.refs_3_
  42.6 0.0 collective-permute-done.refs_0_
  42.6 0.0 collective-permute-done.5.refs_5_
  42.6 0.6 shard_map.59
  43.2 6.0 %collective-permute-start.6 = (f32[13,8,128]{2,1,0:T(8,128)S(1)}, f32[13,8,128]{2,1,0:T(8,128)S(1)}, u32[]{:S(2)}, u32[]{:S(2)}) collective-permute-start(f32[13,8,128]{2,1,0:T(8,128)S(1)} %get-tuple-element.48), channel_id=1, source_target_pairs={{0,896},{128,256},{256,128},{384,512},{512,384},{640,768},{768,640... | collective-permute-start | bytes 159752 | tf_op jit(solution)/shard_map/ppermute | solution.py:636
  49.2 5.1 %collective-permute-start.9 = (f32[13,8,128]{2,1,0:T(8,128)S(1)}, f32[13,8,128]{2,1,0:T(8,128)S(1)}, u32[]{:S(2)}, u32[]{:S(2)}) collective-permute-start(f32[13,8,128]{2,1,0:T(8,128)S(1)} %get-tuple-element.51), channel_id=1, source_target_pairs={{0,128},{128,0},{256,384},{384,256},{512,640},{640,512},{768,896},... | collective-permute-start | bytes 159752 | tf_op jit(solution)/shard_map/ppermute | solution.py:636
  54.4 3.0 %collective-permute-start.7 = (f32[13,4,128]{2,1,0:T(4,128)S(1)}, f32[13,4,128]{2,1,0:T(4,128)S(1)}, u32[]{:S(2)}, u32[]{:S(2)}) collective-permute-start(f32[13,4,128]{2,1,0:T(4,128)S(1)} %get-tuple-element.49), channel_id=1, source_target_pairs={{0,96},{32,64},{64,32},{96,0},{1,97},{33,65},{65,33},{97,1},{2,98}... | collective-permute-start | bytes 79880 | tf_op jit(solution)/shard_map/ppermute | solution.py:636
  57.4 2.6 %collective-permute-start.8 = (f32[13,4,128]{2,1,0:T(4,128)S(1)}, f32[13,4,128]{2,1,0:T(4,128)S(1)}, u32[]{:S(2)}, u32[]{:S(2)}) collective-permute-start(f32[13,4,128]{2,1,0:T(4,128)S(1)} %get-tuple-element.50), channel_id=1, source_target_pairs={{0,32},{32,0},{64,96},{96,64},{1,33},{33,1},{65,97},{97,65},{2,34}... | collective-permute-start | bytes 79880 | tf_op jit(solution)/shard_map/ppermute | solution.py:636
  60.0 1.3 collective-permute-done.7.yo
  61.3 1.8 %collective-permute-done.8.yp = f32[13,4,128]{2,1,0:T(4,128)S(1)} collective-permute-done((f32[13,4,128]{2,1,0:T(4,128)S(1)}, f32[13,4,128]{2,1,0:T(4,128)S(1)}, u32[]{:S(2)}, u32[]{:S(2)}) %collective-permute-start.8) | collective-permute-done | bytes 26656 | tf_op jit(solution)/shard_map/ppermute | solution.py:636
  63.2 0.0 collective-permute-done.6.xo
  63.2 0.0 collective-permute-done.9.xp
  63.2 0.3 shard_map.60
  63.4 4.0 %collective-permute-start.10 = (f32[10,128]{1,0:T(8,128)S(1)}, f32[10,128]{1,0:T(8,128)S(1)}, u32[]{:S(2)}, u32[]{:S(2)}) collective-permute-start(f32[10,128]{1,0:T(8,128)S(1)} %get-tuple-element.55), channel_id=1, source_target_pairs={{0,96},{32,64},{64,32},{96,0},{1,97},{33,65},{65,33},{97,1},{2,98}... | collective-permute-start | bytes 15368 | tf_op jit(solution)/shard_map/ppermute | solution.py:636
  67.5 2.5 %collective-permute-start.12 = (f32[10,128]{1,0:T(8,128)S(1)}, f32[10,128]{1,0:T(8,128)S(1)}, u32[]{:S(2)}, u32[]{:S(2)}) collective-permute-start(f32[10,128]{1,0:T(8,128)S(1)} %get-tuple-element.57), channel_id=1, source_target_pairs={{0,32},{32,0},{64,96},{96,64},{1,33},{33,1},{65,97},{97,65},{2,34}... | collective-permute-start | bytes 15368 | tf_op jit(solution)/shard_map/ppermute | solution.py:636
  70.0 4.3 %collective-permute-start.11 = (f32[8,128]{1,0:T(8,128)S(1)}, f32[8,128]{1,0:T(8,128)S(1)}, u32[]{:S(2)}, u32[]{:S(2)}) collective-permute-start(f32[8,128]{1,0:T(8,128)S(1)} %get-tuple-element.56), channel_id=1, source_target_pairs={{0,31},{1,2},{2,1},{3,4},{4,3},{5,6},{6,5},{7,8},{8,7},{9,10},{10,... | collective-permute-start | bytes 12296 | tf_op jit(solution)/shard_map/ppermute | solution.py:636
  74.3 5.0 %collective-permute-start.13 = (f32[8,128]{1,0:T(8,128)S(1)}, f32[8,128]{1,0:T(8,128)S(1)}, u32[]{:S(2)}, u32[]{:S(2)}) collective-permute-start(f32[8,128]{1,0:T(8,128)S(1)} %get-tuple-element.58), channel_id=1, source_target_pairs={{0,1},{1,0},{2,3},{3,2},{4,5},{5,4},{6,7},{7,6},{8,9},{9,8},{10,11... | collective-permute-start | bytes 12296 | tf_op jit(solution)/shard_map/ppermute | solution.py:636
  79.3 0.0 collective-permute-done.11.zo
  79.3 1.6 %collective-permute-done.13.zp = f32[8,128]{1,0:T(8,128)S(1)} collective-permute-done((f32[8,128]{1,0:T(8,128)S(1)}, f32[8,128]{1,0:T(8,128)S(1)}, u32[]{:S(2)}, u32[]{:S(2)}) %collective-permute-start.13) | collective-permute-done | bytes 4128 | tf_op jit(solution)/shard_map/ppermute | solution.py:636
  80.8 0.0 collective-permute-done.10.eo
  80.8 0.0 collective-permute-done.12.ep
  80.8 0.5 shard_map.61
  81.4 18.7 %all-gather = f32[4,1,128]{2,1,0:T(1,128)S(1)} all-gather(f32[1,1,128]{2,1,0:T(1,128)S(1)} %bitcast.43), channel_id=1, replica_groups=mesh['gx_0'=4,'gx_1'=2,'gy'=4,'gz_0'=8,'gz_1'=4] {'gx_0'}, dimensions={0}, use_global_device_ids=true | all-gather | bytes 2560 | tf_op jit(solution)/shard_map/all_gather | solution.py:642
  100.1 1.8 %all-gather.1 = f32[2,1,128]{2,1,0:T(1,128)S(1)} all-gather(f32[1,1,128]{2,1,0:T(1,128)S(1)} %fusion.3), channel_id=1, replica_groups=mesh['gx_0'=4,'gx_1'=2,'gy'=4,'gz_0'=8,'gz_1'=4] {'gx_1'}, dimensions={0}, use_global_device_ids=true | all-gather | bytes 1536 | tf_op jit(solution)/shard_map/all_gather | solution.py:642
  101.9 8.4 %all-gather.2 = f32[4,1,128]{2,1,0:T(1,128)S(1)} all-gather(f32[1,1,128]{2,1,0:T(1,128)S(1)} %fusion.2), channel_id=1, replica_groups=mesh['gx_0'=4,'gx_1'=2,'gy'=4,'gz_0'=8,'gz_1'=4] {'gy'}, dimensions={0}, use_global_device_ids=true | all-gather | bytes 2560 | tf_op jit(solution)/shard_map/all_gather | solution.py:642
  110.3 9.0 %all-gather.3 = f32[4,1,128]{2,1,0:T(1,128)S(1)} all-gather(f32[1,1,128]{2,1,0:T(1,128)S(1)} %fusion.1), channel_id=1, replica_groups=mesh['gx_0'=4,'gx_1'=2,'gy'=4,'gz_0'=8,'gz_1'=4] {'gz_1'}, dimensions={0}, use_global_device_ids=true | all-gather | bytes 2560 | tf_op jit(solution)/shard_map/all_gather | solution.py:642
  119.3 13.3 %collective-permute-start.14 = (f32[1,128]{1,0:T(1,128)S(1)}, f32[1,128]{1,0:T(1,128)S(1)}, u32[]{:S(2)}, u32[]{:S(2)}) collective-permute-start(f32[1,128]{1,0:T(1,128)S(1)} %bitcast_select_fusion.2), channel_id=1, source_target_pairs={{0,788},{1,793},{2,798},{3,3},{4,792},{5,797},{6,2},{7,7},{8,796},... | collective-permute-start | bytes 1544 | tf_op jit(solution)/shard_map/ppermute | solution.py:660
  132.7 0.6 copy.6
  133.3 0.6 collective-permute-done.14
  133.9 1.8 %all-gather.4 = f32[2,1,128]{2,1,0:T(1,128)S(1)} all-gather(f32[1,1,128]{2,1,0:T(1,128)S(1)} %bitcast.44), channel_id=1, replica_groups=mesh['gx_0'=4,'gx_1'=2,'gy'=4,'gz_0'=8,'gz_1'=4] {'gx_1'}, dimensions={0}, use_global_device_ids=true | all-gather | bytes 1536 | tf_op jit(solution)/shard_map/all_gather | solution.py:642
  135.8 11.6 %all-gather.5 = f32[4,1,128]{2,1,0:T(1,128)S(1)} all-gather(f32[1,1,128]{2,1,0:T(1,128)S(1)} %fusion), channel_id=1, replica_groups=mesh['gx_0'=4,'gx_1'=2,'gy'=4,'gz_0'=8,'gz_1'=4] {'gz_1'}, dimensions={0}, use_global_device_ids=true | all-gather | bytes 2560 | tf_op jit(solution)/shard_map/all_gather | solution.py:642
  147.4 0.9 shard_map.62
  (12 shorter events, 0.2 us)
Async XLA Ops:
  1.7 40.9 %collective-permute-start = (f32[9,8,128]{2,1,0:T(8,128)S(1)}, f32[9,8,128]{2,1,0:T(8,128)S(1)}, u32[]{:S(2)}, u32[]{:S(2)}) collective-permute-start(f32[9,8,128]{2,1,0:T(8,128)S(1)} %get-tuple-element.38), channel_id=1, source_target_pairs={{0,896},{128,256},{256,128},{384,512},{512,384},{640,768},{768,640... | collective-permute-start | bytes 110600 | tf_op jit(solution)/shard_map/ppermute | solution.py:636
  22.3 20.3 %collective-permute-start.5 = (f32[9,8,128]{2,1,0:T(8,128)S(1)}, f32[9,8,128]{2,1,0:T(8,128)S(1)}, u32[]{:S(2)}, u32[]{:S(2)}) collective-permute-start(f32[9,8,128]{2,1,0:T(8,128)S(1)} %get-tuple-element.43), channel_id=1, source_target_pairs={{0,128},{128,0},{256,384},{384,256},{512,640},{640,512},{768,896},... | collective-permute-start | bytes 110600 | tf_op jit(solution)/shard_map/ppermute | solution.py:636
  24.2 18.4 %collective-permute-start.2 = (f32[9,4,128]{2,1,0:T(4,128)S(1)}, f32[9,4,128]{2,1,0:T(4,128)S(1)}, u32[]{:S(2)}, u32[]{:S(2)}) collective-permute-start(f32[9,4,128]{2,1,0:T(4,128)S(1)} %get-tuple-element.40), channel_id=1, source_target_pairs={{0,96},{32,64},{64,32},{96,0},{1,97},{33,65},{65,33},{97,1},{2,98}... | collective-permute-start | bytes 55304 | tf_op jit(solution)/shard_map/ppermute | solution.py:636
  28.9 13.7 %collective-permute-start.3 = (f32[9,4,128]{2,1,0:T(4,128)S(1)}, f32[9,4,128]{2,1,0:T(4,128)S(1)}, u32[]{:S(2)}, u32[]{:S(2)}) collective-permute-start(f32[9,4,128]{2,1,0:T(4,128)S(1)} %get-tuple-element.41), channel_id=1, source_target_pairs={{0,32},{32,0},{64,96},{96,64},{1,33},{33,1},{65,97},{97,65},{2,34}... | collective-permute-start | bytes 55304 | tf_op jit(solution)/shard_map/ppermute | solution.py:636
  31.1 5.5 %collective-permute-start.1 = (f32[8,128]{1,0:T(8,128)S(1)}, f32[8,128]{1,0:T(8,128)S(1)}, u32[]{:S(2)}, u32[]{:S(2)}) collective-permute-start(f32[8,128]{1,0:T(8,128)S(1)} %get-tuple-element.39), channel_id=1, source_target_pairs={{0,31},{1,2},{2,1},{3,4},{4,3},{5,6},{6,5},{7,8},{8,7},{9,10},{10,... | collective-permute-start | bytes 12296 | tf_op jit(solution)/shard_map/ppermute | solution.py:636
  36.6 6.0 %collective-permute-start.4 = (f32[8,128]{1,0:T(8,128)S(1)}, f32[8,128]{1,0:T(8,128)S(1)}, u32[]{:S(2)}, u32[]{:S(2)}) collective-permute-start(f32[8,128]{1,0:T(8,128)S(1)} %get-tuple-element.42), channel_id=1, source_target_pairs={{0,1},{1,0},{2,3},{3,2},{4,5},{5,4},{6,7},{7,6},{8,9},{9,8},{10,11... | collective-permute-start | bytes 12296 | tf_op jit(solution)/shard_map/ppermute | solution.py:636
  43.2 20.0 %collective-permute-start.6 = (f32[13,8,128]{2,1,0:T(8,128)S(1)}, f32[13,8,128]{2,1,0:T(8,128)S(1)}, u32[]{:S(2)}, u32[]{:S(2)}) collective-permute-start(f32[13,8,128]{2,1,0:T(8,128)S(1)} %get-tuple-element.48), channel_id=1, source_target_pairs={{0,896},{128,256},{256,128},{384,512},{512,384},{640,768},{768,640... | collective-permute-start | bytes 159752 | tf_op jit(solution)/shard_map/ppermute | solution.py:636
  49.2 13.9 %collective-permute-start.9 = (f32[13,8,128]{2,1,0:T(8,128)S(1)}, f32[13,8,128]{2,1,0:T(8,128)S(1)}, u32[]{:S(2)}, u32[]{:S(2)}) collective-permute-start(f32[13,8,128]{2,1,0:T(8,128)S(1)} %get-tuple-element.51), channel_id=1, source_target_pairs={{0,128},{128,0},{256,384},{384,256},{512,640},{640,512},{768,896},... | collective-permute-start | bytes 159752 | tf_op jit(solution)/shard_map/ppermute | solution.py:636
  54.4 7.0 %collective-permute-start.7 = (f32[13,4,128]{2,1,0:T(4,128)S(1)}, f32[13,4,128]{2,1,0:T(4,128)S(1)}, u32[]{:S(2)}, u32[]{:S(2)}) collective-permute-start(f32[13,4,128]{2,1,0:T(4,128)S(1)} %get-tuple-element.49), channel_id=1, source_target_pairs={{0,96},{32,64},{64,32},{96,0},{1,97},{33,65},{65,33},{97,1},{2,98}... | collective-permute-start | bytes 79880 | tf_op jit(solution)/shard_map/ppermute | solution.py:636
  57.4 5.7 %collective-permute-start.8 = (f32[13,4,128]{2,1,0:T(4,128)S(1)}, f32[13,4,128]{2,1,0:T(4,128)S(1)}, u32[]{:S(2)}, u32[]{:S(2)}) collective-permute-start(f32[13,4,128]{2,1,0:T(4,128)S(1)} %get-tuple-element.50), channel_id=1, source_target_pairs={{0,32},{32,0},{64,96},{96,64},{1,33},{33,1},{65,97},{97,65},{2,34}... | collective-permute-start | bytes 79880 | tf_op jit(solution)/shard_map/ppermute | solution.py:636
  63.4 17.4 %collective-permute-start.10 = (f32[10,128]{1,0:T(8,128)S(1)}, f32[10,128]{1,0:T(8,128)S(1)}, u32[]{:S(2)}, u32[]{:S(2)}) collective-permute-start(f32[10,128]{1,0:T(8,128)S(1)} %get-tuple-element.55), channel_id=1, source_target_pairs={{0,96},{32,64},{64,32},{96,0},{1,97},{33,65},{65,33},{97,1},{2,98}... | collective-permute-start | bytes 15368 | tf_op jit(solution)/shard_map/ppermute | solution.py:636
  67.5 13.4 %collective-permute-start.12 = (f32[10,128]{1,0:T(8,128)S(1)}, f32[10,128]{1,0:T(8,128)S(1)}, u32[]{:S(2)}, u32[]{:S(2)}) collective-permute-start(f32[10,128]{1,0:T(8,128)S(1)} %get-tuple-element.57), channel_id=1, source_target_pairs={{0,32},{32,0},{64,96},{96,64},{1,33},{33,1},{65,97},{97,65},{2,34}... | collective-permute-start | bytes 15368 | tf_op jit(solution)/shard_map/ppermute | solution.py:636
  70.0 9.3 %collective-permute-start.11 = (f32[8,128]{1,0:T(8,128)S(1)}, f32[8,128]{1,0:T(8,128)S(1)}, u32[]{:S(2)}, u32[]{:S(2)}) collective-permute-start(f32[8,128]{1,0:T(8,128)S(1)} %get-tuple-element.56), channel_id=1, source_target_pairs={{0,31},{1,2},{2,1},{3,4},{4,3},{5,6},{6,5},{7,8},{8,7},{9,10},{10,... | collective-permute-start | bytes 12296 | tf_op jit(solution)/shard_map/ppermute | solution.py:636
  74.3 6.5 %collective-permute-start.13 = (f32[8,128]{1,0:T(8,128)S(1)}, f32[8,128]{1,0:T(8,128)S(1)}, u32[]{:S(2)}, u32[]{:S(2)}) collective-permute-start(f32[8,128]{1,0:T(8,128)S(1)} %get-tuple-element.58), channel_id=1, source_target_pairs={{0,1},{1,0},{2,3},{3,2},{4,5},{5,4},{6,7},{7,6},{8,9},{9,8},{10,11... | collective-permute-start | bytes 12296 | tf_op jit(solution)/shard_map/ppermute | solution.py:636
  119.3 14.6 %collective-permute-start.14 = (f32[1,128]{1,0:T(1,128)S(1)}, f32[1,128]{1,0:T(1,128)S(1)}, u32[]{:S(2)}, u32[]{:S(2)}) collective-permute-start(f32[1,128]{1,0:T(1,128)S(1)} %bitcast_select_fusion.2), channel_id=1, source_target_pairs={{0,788},{1,793},{2,798},{3,3},{4,792},{5,797},{6,2},{7,7},{8,796},... | collective-permute-start | bytes 1544 | tf_op jit(solution)/shard_map/ppermute | solution.py:660

commit v5 on v3

--- a/solution.py
+++ b/solution.py
@@ -431,9 +431,8 @@
     return [field[first + c][x] for c in range(count)]
 
 
-def join_kernel(f1_ref, f2_ref, xo, yo, yp, xp, f2_out, side_ref, row_ref, zo, eo, ep, zp):
+def side_kernel(f1_ref, f2_ref, xo, xp, f2_out, side_ref, eo, ep):
     even = is_even()
-    y = Line(0)
     f1, f2 = (load(f1_ref), load(f2_ref))
     sides = []
     for low, x, sign in ((True, 0, -6.0), (False, NX - 1, 6.0)):
@@ -444,6 +443,22 @@
             f2[c][x] = value
         side[5:] = meet(side[5:], [-value for value in gap], 0, -sign)
         sides.append(side)
+    for x in range(NX):
+        for c in range(8):
+            f2_out[c, x] = f2[c][x]
+    for w, side in enumerate(sides):
+        for c in range(13):
+            side_ref[w, c] = side[c]
+        for c in range(5):
+            low, high = (side[c][0:1, :], side[c][NY - 1 : NY, :])
+            eo[pl.ds(5 * w + c, 1), :] = jnp.where(even[1], low, high)
+            ep[pl.ds(5 * w + c, 1), :] = jnp.where(even[1], high, low)
+
+
+def join_kernel(f1_ref, f2_ref, side_ref, yo, yp, f2_out, row_ref, zo, zp):
+    even = is_even()
+    y = Line(0)
+    f1, f2 = (load(f1_ref), load(f2_ref))
     outer, sign = ends(y)
     rows = [[None] * NX for _ in range(13)]
     for x in range(NX):
@@ -462,14 +477,8 @@
             f2_out[c, x] = f2[c][x]
         for c in range(13):
             row_ref[c, x] = rows[c][x]
-    for w, side in enumerate(sides):
-        for c in range(13):
-            side_ref[w, c] = side[c]
-        for c in range(5):
-            low, high = (side[c][0:1, :], side[c][NY - 1 : NY, :])
-            eo[pl.ds(5 * w + c, 1), :] = jnp.where(even[1], low, high)
-            ep[pl.ds(5 * w + c, 1), :] = jnp.where(even[1], high, low)
-    pack_z(flat(f1 + f2) + sides[0][:5] + sides[1][:5] + flat(rows[:5]), zo, zp)
+    sides = [side_ref[w, c] for w in range(2) for c in range(5)]
+    pack_z(flat(f1 + f2) + sides + flat(rows[:5]), zo, zp)
 
 
 class Around:
@@ -489,7 +498,7 @@
 
 
 def last_kernel(
-    u_ref, rate_ref, fast_ref, f1_ref, f2_ref, side_ref, row_ref, zo, eo, ep, zp, next_ref, stat_ref
+    u_ref, rate_ref, fast_ref, f1_ref, f2_ref, side_ref, row_ref, eo, ep, zo, zp, next_ref, stat_ref
 ):
     even = is_even()
     y, z = (Line(0), Line(1))
@@ -625,7 +634,8 @@
         (GX, pair_of),
     ),
     "second": ((GX, other_of), ("gy", other_of), ("gy", pair_of), (GX, pair_of)),
-    "third": ((GZ, other_of), ("gy", other_of), ("gy", pair_of), (GZ, pair_of)),
+    "corner": (("gy", other_of), ("gy", pair_of)),
+    "third": ((GZ, other_of), (GZ, pair_of)),
 }
 
 
@@ -697,16 +707,18 @@
         [shape(5, *full), shape(5, *full), shape(8, *full), planes, rows, rows, planes],
         10**6,
     )(u, g, vol, alpha, *received)
-    received = exchange(messages, "second")
+    xo, yo, yp, xp = exchange(messages, "second")
     corners = shape(10, NZ)
-    f2, sides, rows, *messages = call(
-        join_kernel,
-        [shape(8, *full), shape(2, 13, NY, NZ), shape(13, *full), tile, corners, corners, tile],
-        10**6,
-    )(f1, f2, *received)
+    f2, sides, *messages = call(
+        side_kernel, [shape(8, *full), shape(2, 13, NY, NZ), corners, corners], 10**6
+    )(f1, f2, xo, xp)
+    corners = exchange(messages, "corner")
+    f2, rows, *messages = call(
+        join_kernel, [shape(8, *full), shape(13, *full), tile, tile], 10**6
+    )(f1, f2, sides, yo, yp)
     received = exchange(messages, "third")
     field, stat = call(last_kernel, [shape(8, *full), shape(1, NZ)], 10**6)(
-        u, rate, fast, f1, f2, sides, rows, *received
+        u, rate, fast, f1, f2, sides, rows, *corners, *received
     )
     stat = over_all(stat)
     gravity, gravity_source, norm = call(

time: 149 us -> 147 us (0.987)
  the two profiles are of different devices: /device:TPU:72 before, /device:TPU:8 now
where the time goes in v5:
time: 147 us; the launch traced here: 146 us
  starting transfers between devices  83.1 us (57%)
  blocking collectives  48.8 us (33%)
  waiting for transfers between devices  8.51 us (6%)
  Pallas kernels  3.84 us (3%)
    ppermute x14, starting transfers between devices, exchange(): lax.ppermute(message, axis, [(a, partner(a, size)) for a in range(size)])  81.2 us
    all_gather x6, blocking collectives, gather(): every = lax.all_gather(stat, axis, tiled=True)  48.8 us
    ppermute x14, waiting for transfers between devices, exchange(): lax.ppermute(message, axis, [(a, partner(a, size)) for a in range(size)])  4.72 us
    pallas_call x7, Pallas kernels, run(): pl.pallas_call(kernel, in_specs=[pl.BlockSpec(memory_space=pltpu.VMEM)] *...  3.84 us
    ppermute x1, waiting for transfers between devices, spread(): return lax.ppermute(stat, names, pairs)  3.79 us
  transfers between devices with their start and end apart: 15, of which 4 were waited for; matrix products, arithmetic and copies ran while one was open for 0% of the time, Pallas kernels for 1%

profile of v5, /device:TPU:8, one launch (start us, length us, event | category | flops | bytes accessed | tf_op | source)
XLA Modules:
  0.0 145.9 jit_solution(14976739870771342858)
XLA Ops:
  0.6 1.0 shard_map.57
  1.7 22.4 %collective-permute-start = (f32[9,8,128]{2,1,0:T(8,128)S(1)}, f32[9,8,128]{2,1,0:T(8,128)S(1)}, u32[]{:S(2)}, u32[]{:S(2)}) collective-permute-start(f32[9,8,128]{2,1,0:T(8,128)S(1)} %get-tuple-element.39), channel_id=1, source_target_pairs={{0,896},{128,256},{256,128},{384,512},{512,384},{640,768},{768,640... | collective-permute-start | bytes 110600 | tf_op jit(solution)/shard_map/ppermute | solution.py:646
  24.1 1.9 %collective-permute-start.5 = (f32[9,8,128]{2,1,0:T(8,128)S(1)}, f32[9,8,128]{2,1,0:T(8,128)S(1)}, u32[]{:S(2)}, u32[]{:S(2)}) collective-permute-start(f32[9,8,128]{2,1,0:T(8,128)S(1)} %get-tuple-element.44), channel_id=1, source_target_pairs={{0,128},{128,0},{256,384},{384,256},{512,640},{640,512},{768,896},... | collective-permute-start | bytes 110600 | tf_op jit(solution)/shard_map/ppermute | solution.py:646
  26.0 4.7 %collective-permute-start.2 = (f32[9,4,128]{2,1,0:T(4,128)S(1)}, f32[9,4,128]{2,1,0:T(4,128)S(1)}, u32[]{:S(2)}, u32[]{:S(2)}) collective-permute-start(f32[9,4,128]{2,1,0:T(4,128)S(1)} %get-tuple-element.41), channel_id=1, source_target_pairs={{0,96},{32,64},{64,32},{96,0},{1,97},{33,65},{65,33},{97,1},{2,98}... | collective-permute-start | bytes 55304 | tf_op jit(solution)/shard_map/ppermute | solution.py:646
  30.7 2.1 %collective-permute-start.3 = (f32[9,4,128]{2,1,0:T(4,128)S(1)}, f32[9,4,128]{2,1,0:T(4,128)S(1)}, u32[]{:S(2)}, u32[]{:S(2)}) collective-permute-start(f32[9,4,128]{2,1,0:T(4,128)S(1)} %get-tuple-element.42), channel_id=1, source_target_pairs={{0,32},{32,0},{64,96},{96,64},{1,33},{33,1},{65,97},{97,65},{2,34}... | collective-permute-start | bytes 55304 | tf_op jit(solution)/shard_map/ppermute | solution.py:646
  32.9 3.5 %collective-permute-start.1 = (f32[8,128]{1,0:T(8,128)S(1)}, f32[8,128]{1,0:T(8,128)S(1)}, u32[]{:S(2)}, u32[]{:S(2)}) collective-permute-start(f32[8,128]{1,0:T(8,128)S(1)} %get-tuple-element.40), channel_id=1, source_target_pairs={{0,31},{1,2},{2,1},{3,4},{4,3},{5,6},{6,5},{7,8},{8,7},{9,10},{10,... | collective-permute-start | bytes 12296 | tf_op jit(solution)/shard_map/ppermute | solution.py:646
  36.4 2.0 %collective-permute-done.1.refs_1_ = f32[8,128]{1,0:T(8,128)S(1)} collective-permute-done((f32[8,128]{1,0:T(8,128)S(1)}, f32[8,128]{1,0:T(8,128)S(1)}, u32[]{:S(2)}, u32[]{:S(2)}) %collective-permute-start.1) | collective-permute-done | bytes 4128 | tf_op jit(solution)/shard_map/ppermute | solution.py:646
  38.4 11.1 %collective-permute-start.4 = (f32[8,128]{1,0:T(8,128)S(1)}, f32[8,128]{1,0:T(8,128)S(1)}, u32[]{:S(2)}, u32[]{:S(2)}) collective-permute-start(f32[8,128]{1,0:T(8,128)S(1)} %get-tuple-element.43), channel_id=1, source_target_pairs={{0,1},{1,0},{2,3},{3,2},{4,5},{5,4},{6,7},{7,6},{8,9},{9,8},{10,11... | collective-permute-start | bytes 12296 | tf_op jit(solution)/shard_map/ppermute | solution.py:646
  49.4 0.4 shard_map.58
  49.9 1.1 collective-permute-done.4.refs_4_
  51.0 0.0 collective-permute-done.2.refs_2_
  51.0 0.0 collective-permute-done.3.refs_3_
  51.0 0.0 collective-permute-done.refs_0_
  51.0 0.0 collective-permute-done.5.refs_5_
  51.0 0.6 shard_map.59
  51.6 6.0 %collective-permute-start.6 = (f32[13,8,128]{2,1,0:T(8,128)S(1)}, f32[13,8,128]{2,1,0:T(8,128)S(1)}, u32[]{:S(2)}, u32[]{:S(2)}) collective-permute-start(f32[13,8,128]{2,1,0:T(8,128)S(1)} %get-tuple-element.49), channel_id=1, source_target_pairs={{0,896},{128,256},{256,128},{384,512},{512,384},{640,768},{768,640... | collective-permute-start | bytes 159752 | tf_op jit(solution)/shard_map/ppermute | solution.py:646
  57.7 5.1 %collective-permute-start.7 = (f32[13,8,128]{2,1,0:T(8,128)S(1)}, f32[13,8,128]{2,1,0:T(8,128)S(1)}, u32[]{:S(2)}, u32[]{:S(2)}) collective-permute-start(f32[13,8,128]{2,1,0:T(8,128)S(1)} %get-tuple-element.50), channel_id=1, source_target_pairs={{0,128},{128,0},{256,384},{384,256},{512,640},{640,512},{768,896},... | collective-permute-start | bytes 159752 | tf_op jit(solution)/shard_map/ppermute | solution.py:646
  62.8 3.0 %collective-permute-start.8 = (f32[13,4,128]{2,1,0:T(4,128)S(1)}, f32[13,4,128]{2,1,0:T(4,128)S(1)}, u32[]{:S(2)}, u32[]{:S(2)}) collective-permute-start(f32[13,4,128]{2,1,0:T(4,128)S(1)} %get-tuple-element.53), channel_id=1, source_target_pairs={{0,96},{32,64},{64,32},{96,0},{1,97},{33,65},{65,33},{97,1},{2,98}... | collective-permute-start | bytes 79880 | tf_op jit(solution)/shard_map/ppermute | solution.py:646
  65.8 2.6 %collective-permute-start.9 = (f32[13,4,128]{2,1,0:T(4,128)S(1)}, f32[13,4,128]{2,1,0:T(4,128)S(1)}, u32[]{:S(2)}, u32[]{:S(2)}) collective-permute-start(f32[13,4,128]{2,1,0:T(4,128)S(1)} %get-tuple-element.54), channel_id=1, source_target_pairs={{0,32},{32,0},{64,96},{96,64},{1,33},{33,1},{65,97},{97,65},{2,34}... | collective-permute-start | bytes 79880 | tf_op jit(solution)/shard_map/ppermute | solution.py:646
  68.4 0.0 collective-permute-done.6.xo
  68.4 0.0 collective-permute-done.7.xp
  68.5 4.5 %collective-permute-start.10 = (f32[10,128]{1,0:T(8,128)S(1)}, f32[10,128]{1,0:T(8,128)S(1)}, u32[]{:S(2)}, u32[]{:S(2)}) collective-permute-start(f32[10,128]{1,0:T(8,128)S(1)} %get-tuple-element.57), channel_id=1, source_target_pairs={{0,96},{32,64},{64,32},{96,0},{1,97},{33,65},{65,33},{97,1},{2,98}... | collective-permute-start | bytes 15368 | tf_op jit(solution)/shard_map/ppermute | solution.py:646
  73.0 2.1 %collective-permute-start.11 = (f32[10,128]{1,0:T(8,128)S(1)}, f32[10,128]{1,0:T(8,128)S(1)}, u32[]{:S(2)}, u32[]{:S(2)}) collective-permute-start(f32[10,128]{1,0:T(8,128)S(1)} %get-tuple-element.58), channel_id=1, source_target_pairs={{0,32},{32,0},{64,96},{96,64},{1,33},{33,1},{65,97},{97,65},{2,34}... | collective-permute-start | bytes 15368 | tf_op jit(solution)/shard_map/ppermute | solution.py:646
  75.2 0.0 collective-permute-done.8.yo
  75.2 0.0 collective-permute-done.9.yp
  75.2 0.3 shard_map.61
  75.4 1.9 %collective-permute-start.12 = (f32[8,128]{1,0:T(8,128)S(1)}, f32[8,128]{1,0:T(8,128)S(1)}, u32[]{:S(2)}, u32[]{:S(2)}) collective-permute-start(f32[8,128]{1,0:T(8,128)S(1)} %get-tuple-element.59), channel_id=1, source_target_pairs={{0,31},{1,2},{2,1},{3,4},{4,3},{5,6},{6,5},{7,8},{8,7},{9,10},{10,... | collective-permute-start | bytes 12296 | tf_op jit(solution)/shard_map/ppermute | solution.py:646
  77.4 10.1 %collective-permute-start.13 = (f32[8,128]{1,0:T(8,128)S(1)}, f32[8,128]{1,0:T(8,128)S(1)}, u32[]{:S(2)}, u32[]{:S(2)}) collective-permute-start(f32[8,128]{1,0:T(8,128)S(1)} %get-tuple-element.60), channel_id=1, source_target_pairs={{0,1},{1,0},{2,3},{3,2},{4,5},{5,4},{6,7},{7,6},{8,9},{9,8},{10,11... | collective-permute-start | bytes 12296 | tf_op jit(solution)/shard_map/ppermute | solution.py:646
  87.5 0.0 collective-permute-done.12.zo
  87.5 1.6 %collective-permute-done.13.zp = f32[8,128]{1,0:T(8,128)S(1)} collective-permute-done((f32[8,128]{1,0:T(8,128)S(1)}, f32[8,128]{1,0:T(8,128)S(1)}, u32[]{:S(2)}, u32[]{:S(2)}) %collective-permute-start.13) | collective-permute-done | bytes 4128 | tf_op jit(solution)/shard_map/ppermute | solution.py:646
  89.1 0.0 collective-permute-done.10.eo
  89.1 0.0 collective-permute-done.11.ep
  89.1 0.5 shard_map.62
  89.6 18.9 %all-gather = f32[4,1,128]{2,1,0:T(1,128)S(1)} all-gather(f32[1,1,128]{2,1,0:T(1,128)S(1)} %bitcast.43), channel_id=1, replica_groups=mesh['gx_0'=4,'gx_1'=2,'gy'=4,'gz_0'=8,'gz_1'=4] {'gx_0'}, dimensions={0}, use_global_device_ids=true | all-gather | bytes 2560 | tf_op jit(solution)/shard_map/all_gather | solution.py:652
  108.5 1.8 %all-gather.1 = f32[2,1,128]{2,1,0:T(1,128)S(1)} all-gather(f32[1,1,128]{2,1,0:T(1,128)S(1)} %fusion.3), channel_id=1, replica_groups=mesh['gx_0'=4,'gx_1'=2,'gy'=4,'gz_0'=8,'gz_1'=4] {'gx_1'}, dimensions={0}, use_global_device_ids=true | all-gather | bytes 1536 | tf_op jit(solution)/shard_map/all_gather | solution.py:652
  110.4 9.5 %all-gather.2 = f32[4,1,128]{2,1,0:T(1,128)S(1)} all-gather(f32[1,1,128]{2,1,0:T(1,128)S(1)} %fusion.2), channel_id=1, replica_groups=mesh['gx_0'=4,'gx_1'=2,'gy'=4,'gz_0'=8,'gz_1'=4] {'gy'}, dimensions={0}, use_global_device_ids=true | all-gather | bytes 2560 | tf_op jit(solution)/shard_map/all_gather | solution.py:652
  119.9 9.0 %all-gather.3 = f32[4,1,128]{2,1,0:T(1,128)S(1)} all-gather(f32[1,1,128]{2,1,0:T(1,128)S(1)} %fusion.1), channel_id=1, replica_groups=mesh['gx_0'=4,'gx_1'=2,'gy'=4,'gz_0'=8,'gz_1'=4] {'gz_1'}, dimensions={0}, use_global_device_ids=true | all-gather | bytes 2560 | tf_op jit(solution)/shard_map/all_gather | solution.py:652
  128.9 1.9 %collective-permute-start.14 = (f32[1,128]{1,0:T(1,128)S(1)}, f32[1,128]{1,0:T(1,128)S(1)}, u32[]{:S(2)}, u32[]{:S(2)}) collective-permute-start(f32[1,128]{1,0:T(1,128)S(1)} %bitcast_select_fusion.2), channel_id=1, source_target_pairs={{0,788},{1,793},{2,798},{3,3},{4,792},{5,797},{6,2},{7,7},{8,796},... | collective-permute-start | bytes 1544 | tf_op jit(solution)/shard_map/ppermute | solution.py:670
  130.8 0.6 copy.6
  131.4 3.8 %collective-permute-done.14 = f32[1,128]{1,0:T(1,128)S(1)} collective-permute-done((f32[1,128]{1,0:T(1,128)S(1)}, f32[1,128]{1,0:T(1,128)S(1)}, u32[]{:S(2)}, u32[]{:S(2)}) %collective-permute-start.14) | collective-permute-done | bytes 544 | tf_op jit(solution)/shard_map/ppermute | solution.py:670
  135.2 1.8 %all-gather.4 = f32[2,1,128]{2,1,0:T(1,128)S(1)} all-gather(f32[1,1,128]{2,1,0:T(1,128)S(1)} %bitcast.44), channel_id=1, replica_groups=mesh['gx_0'=4,'gx_1'=2,'gy'=4,'gz_0'=8,'gz_1'=4] {'gx_1'}, dimensions={0}, use_global_device_ids=true | all-gather | bytes 1536 | tf_op jit(solution)/shard_map/all_gather | solution.py:652
  137.1 7.9 %all-gather.5 = f32[4,1,128]{2,1,0:T(1,128)S(1)} all-gather(f32[1,1,128]{2,1,0:T(1,128)S(1)} %fusion), channel_id=1, replica_groups=mesh['gx_0'=4,'gx_1'=2,'gy'=4,'gz_0'=8,'gz_1'=4] {'gz_1'}, dimensions={0}, use_global_device_ids=true | all-gather | bytes 2560 | tf_op jit(solution)/shard_map/all_gather | solution.py:652
  145.0 1.0 shard_map.63
  (13 shorter events, 0.2 us)
Async XLA Ops:
  1.7 49.3 %collective-permute-start = (f32[9,8,128]{2,1,0:T(8,128)S(1)}, f32[9,8,128]{2,1,0:T(8,128)S(1)}, u32[]{:S(2)}, u32[]{:S(2)}) collective-permute-start(f32[9,8,128]{2,1,0:T(8,128)S(1)} %get-tuple-element.39), channel_id=1, source_target_pairs={{0,896},{128,256},{256,128},{384,512},{512,384},{640,768},{768,640... | collective-permute-start | bytes 110600 | tf_op jit(solution)/shard_map/ppermute | solution.py:646
  24.1 26.9 %collective-permute-start.5 = (f32[9,8,128]{2,1,0:T(8,128)S(1)}, f32[9,8,128]{2,1,0:T(8,128)S(1)}, u32[]{:S(2)}, u32[]{:S(2)}) collective-permute-start(f32[9,8,128]{2,1,0:T(8,128)S(1)} %get-tuple-element.44), channel_id=1, source_target_pairs={{0,128},{128,0},{256,384},{384,256},{512,640},{640,512},{768,896},... | collective-permute-start | bytes 110600 | tf_op jit(solution)/shard_map/ppermute | solution.py:646
  26.0 25.0 %collective-permute-start.2 = (f32[9,4,128]{2,1,0:T(4,128)S(1)}, f32[9,4,128]{2,1,0:T(4,128)S(1)}, u32[]{:S(2)}, u32[]{:S(2)}) collective-permute-start(f32[9,4,128]{2,1,0:T(4,128)S(1)} %get-tuple-element.41), channel_id=1, source_target_pairs={{0,96},{32,64},{64,32},{96,0},{1,97},{33,65},{65,33},{97,1},{2,98}... | collective-permute-start | bytes 55304 | tf_op jit(solution)/shard_map/ppermute | solution.py:646
  30.7 20.3 %collective-permute-start.3 = (f32[9,4,128]{2,1,0:T(4,128)S(1)}, f32[9,4,128]{2,1,0:T(4,128)S(1)}, u32[]{:S(2)}, u32[]{:S(2)}) collective-permute-start(f32[9,4,128]{2,1,0:T(4,128)S(1)} %get-tuple-element.42), channel_id=1, source_target_pairs={{0,32},{32,0},{64,96},{96,64},{1,33},{33,1},{65,97},{97,65},{2,34}... | collective-permute-start | bytes 55304 | tf_op jit(solution)/shard_map/ppermute | solution.py:646
  32.9 5.5 %collective-permute-start.1 = (f32[8,128]{1,0:T(8,128)S(1)}, f32[8,128]{1,0:T(8,128)S(1)}, u32[]{:S(2)}, u32[]{:S(2)}) collective-permute-start(f32[8,128]{1,0:T(8,128)S(1)} %get-tuple-element.40), channel_id=1, source_target_pairs={{0,31},{1,2},{2,1},{3,4},{4,3},{5,6},{6,5},{7,8},{8,7},{9,10},{10,... | collective-permute-start | bytes 12296 | tf_op jit(solution)/shard_map/ppermute | solution.py:646
  38.4 12.6 %collective-permute-start.4 = (f32[8,128]{1,0:T(8,128)S(1)}, f32[8,128]{1,0:T(8,128)S(1)}, u32[]{:S(2)}, u32[]{:S(2)}) collective-permute-start(f32[8,128]{1,0:T(8,128)S(1)} %get-tuple-element.43), channel_id=1, source_target_pairs={{0,1},{1,0},{2,3},{3,2},{4,5},{5,4},{6,7},{7,6},{8,9},{9,8},{10,11... | collective-permute-start | bytes 12296 | tf_op jit(solution)/shard_map/ppermute | solution.py:646
  51.6 16.8 %collective-permute-start.6 = (f32[13,8,128]{2,1,0:T(8,128)S(1)}, f32[13,8,128]{2,1,0:T(8,128)S(1)}, u32[]{:S(2)}, u32[]{:S(2)}) collective-permute-start(f32[13,8,128]{2,1,0:T(8,128)S(1)} %get-tuple-element.49), channel_id=1, source_target_pairs={{0,896},{128,256},{256,128},{384,512},{512,384},{640,768},{768,640... | collective-permute-start | bytes 159752 | tf_op jit(solution)/shard_map/ppermute | solution.py:646
  57.7 10.8 %collective-permute-start.7 = (f32[13,8,128]{2,1,0:T(8,128)S(1)}, f32[13,8,128]{2,1,0:T(8,128)S(1)}, u32[]{:S(2)}, u32[]{:S(2)}) collective-permute-start(f32[13,8,128]{2,1,0:T(8,128)S(1)} %get-tuple-element.50), channel_id=1, source_target_pairs={{0,128},{128,0},{256,384},{384,256},{512,640},{640,512},{768,896},... | collective-permute-start | bytes 159752 | tf_op jit(solution)/shard_map/ppermute | solution.py:646
  62.8 12.4 %collective-permute-start.8 = (f32[13,4,128]{2,1,0:T(4,128)S(1)}, f32[13,4,128]{2,1,0:T(4,128)S(1)}, u32[]{:S(2)}, u32[]{:S(2)}) collective-permute-start(f32[13,4,128]{2,1,0:T(4,128)S(1)} %get-tuple-element.53), channel_id=1, source_target_pairs={{0,96},{32,64},{64,32},{96,0},{1,97},{33,65},{65,33},{97,1},{2,98}... | collective-permute-start | bytes 79880 | tf_op jit(solution)/shard_map/ppermute | solution.py:646
  65.8 9.4 %collective-permute-start.9 = (f32[13,4,128]{2,1,0:T(4,128)S(1)}, f32[13,4,128]{2,1,0:T(4,128)S(1)}, u32[]{:S(2)}, u32[]{:S(2)}) collective-permute-start(f32[13,4,128]{2,1,0:T(4,128)S(1)} %get-tuple-element.54), channel_id=1, source_target_pairs={{0,32},{32,0},{64,96},{96,64},{1,33},{33,1},{65,97},{97,65},{2,34}... | collective-permute-start | bytes 79880 | tf_op jit(solution)/shard_map/ppermute | solution.py:646
  68.5 20.6 %collective-permute-start.10 = (f32[10,128]{1,0:T(8,128)S(1)}, f32[10,128]{1,0:T(8,128)S(1)}, u32[]{:S(2)}, u32[]{:S(2)}) collective-permute-start(f32[10,128]{1,0:T(8,128)S(1)} %get-tuple-element.57), channel_id=1, source_target_pairs={{0,96},{32,64},{64,32},{96,0},{1,97},{33,65},{65,33},{97,1},{2,98}... | collective-permute-start | bytes 15368 | tf_op jit(solution)/shard_map/ppermute | solution.py:646
  73.0 16.1 %collective-permute-start.11 = (f32[10,128]{1,0:T(8,128)S(1)}, f32[10,128]{1,0:T(8,128)S(1)}, u32[]{:S(2)}, u32[]{:S(2)}) collective-permute-start(f32[10,128]{1,0:T(8,128)S(1)} %get-tuple-element.58), channel_id=1, source_target_pairs={{0,32},{32,0},{64,96},{96,64},{1,33},{33,1},{65,97},{97,65},{2,34}... | collective-permute-start | bytes 15368 | tf_op jit(solution)/shard_map/ppermute | solution.py:646
  75.4 12.0 %collective-permute-start.12 = (f32[8,128]{1,0:T(8,128)S(1)}, f32[8,128]{1,0:T(8,128)S(1)}, u32[]{:S(2)}, u32[]{:S(2)}) collective-permute-start(f32[8,128]{1,0:T(8,128)S(1)} %get-tuple-element.59), channel_id=1, source_target_pairs={{0,31},{1,2},{2,1},{3,4},{4,3},{5,6},{6,5},{7,8},{8,7},{9,10},{10,... | collective-permute-start | bytes 12296 | tf_op jit(solution)/shard_map/ppermute | solution.py:646
  77.4 11.7 %collective-permute-start.13 = (f32[8,128]{1,0:T(8,128)S(1)}, f32[8,128]{1,0:T(8,128)S(1)}, u32[]{:S(2)}, u32[]{:S(2)}) collective-permute-start(f32[8,128]{1,0:T(8,128)S(1)} %get-tuple-element.60), channel_id=1, source_target_pairs={{0,1},{1,0},{2,3},{3,2},{4,5},{5,4},{6,7},{7,6},{8,9},{9,8},{10,11... | collective-permute-start | bytes 12296 | tf_op jit(solution)/shard_map/ppermute | solution.py:646
  128.9 6.4 %collective-permute-start.14 = (f32[1,128]{1,0:T(1,128)S(1)}, f32[1,128]{1,0:T(1,128)S(1)}, u32[]{:S(2)}, u32[]{:S(2)}) collective-permute-start(f32[1,128]{1,0:T(1,128)S(1)} %bitcast_select_fusion.2), channel_id=1, source_target_pairs={{0,788},{1,793},{2,798},{3,3},{4,792},{5,797},{6,2},{7,7},{8,796},... | collective-permute-start | bytes 1544 | tf_op jit(solution)/shard_map/ppermute | solution.py:670
